TPU v7x, 128 devices: a whole 4x4x4 slice. The times are simulated.
128 devices in a mesh: gx: 8 (over y, core), gy: 16 (over z, x).
Axes of the slice: x: 4, y: 4, z: 4, core: 2. Of those that a mesh axis runs over, the one named last changes fastest.
Arguments:
- spectra: bfloat16 [8, 16, 3, 2, 128, 4096], P('gx', 'gy'), may hold values from -1000 to 1000
- partner_codes: int32 [8, 16, 5], P('gx', 'gy'), may hold values from -1 to 4, as said below
- range_bits: int32 [8, 16, 5, 128, 5], P('gx', 'gy'), may hold values from 0 to 1073741823
- old_stacks: float32 [8, 16, 5, 8, 2, 128, 128], P('gx', 'gy'), may hold values from -6 to 6
Outputs:
- stacks: float32 [8, 16, 5, 8, 2, 128, 128], P('gx', 'gy')
Inputs may be any that keep to these rules, and one draw needn't show every extreme that they name: `partner_codes`: each block lists code 0 first, then further distinct codes in increasing order, then -1 in the remaining slots; no listed code names a block outside the grid of 8 x 16 blocks; some block lists all 5 codes.
All inputs are finite; a program needn't handle non-finite values.
Results may differ from a plain program's by a relative error of at most 0.0014.
Values may be sent and summed in bfloat16 or wider, within the bound.
A program may use at most 192 MiB of HBM per device.

v0:
```python
import math

import jax
import jax.numpy as jnp
from jax import lax
from jax.experimental import pallas as pl
from jax.experimental.pallas import tpu as pltpu
from jax.sharding import PartitionSpec as P

EPSILON = 1e-06
MESH = pl.DeviceIdType.MESH
ROWS = 8
COLS = 16
ST = 128
SEG = 3
BANDS = 8
BW = 512
SLOTS = 5
WORDS = 5
SCALE = 1.0 / math.sqrt(SEG * BW)

OWN, OTHER, UPPER, LOWER, LEFT, RIGHT, PLACES = 0, 8, 12, 16, 20, 24, 28


def whiten(w, place):
    def rows_of(t, carry):
        first = pl.multiple_of(t * 16, 16)
        total = jnp.zeros((16, BW), jnp.float32)
        for s in range(SEG):
            for c in range(2):
                x = w[place, s, pl.ds(c * ST + first, 16), :].astype(jnp.float32)
                total = total + x * x
        power = jnp.sum(total, axis=-1, keepdims=True) * (1.0 / (SEG * 2 * BW))
        gain = lax.rsqrt(power + EPSILON)
        for s in range(SEG):
            for c in range(2):
                x = w[place, s, pl.ds(c * ST + first, 16), :].astype(jnp.float32)
                w[place, s, pl.ds(c * ST + first, 16), :] = (x * gain).astype(jnp.bfloat16)
        return carry

    lax.fori_loop(0, ST // 16, rows_of, 0)


def pair(w, x, y):
    total = None
    for s in range(SEG):
        part = lax.dot_general(
            w[x, s], w[y, s], (((1,), (1,)), ((), ())), preferred_element_type=jnp.float32
        )
        total = part if total is None else total + part
    real = (total[:ST, :ST] + total[ST:, ST:]) * SCALE
    imag = (total[ST:, :ST] - total[:ST, ST:]) * SCALE
    return real, imag


def kernel(
    codes, bits, spectra, old, out,
    w, cross, keep, mask, pick, sent_p, got_p, sent_q, got_q,
    load_sem, old_sem, out_sem,
    die_s, die_r, row_s, row_r, col_s, col_r,
    p_s, p_r, q_s, q_r, e_s, e_r, d_s, d_r,
):
    gx = lax.axis_index("gx")
    gy = lax.axis_index("gy")
    k = lax.rem(gx, 2)
    o = 1 - k
    base = gx - k
    right = lax.rem(gy + 1, COLS)
    left = lax.rem(gy + COLS - 1, COLS)
    above = lax.rem(base + ROWS - 2, ROWS)
    below = lax.rem(base + 2, ROWS)

    def band(b):
        return spectra.at[:, :, pl.ds(pl.multiple_of(b * BW, BW), BW)]

    def remote(src, dst, send, recv, row, col):
        return pltpu.make_async_remote_copy(
            src_ref=src, dst_ref=dst, send_sem=send, recv_sem=recv,
            device_id=(row, col), device_id_type=MESH,
        )

    def load(b):
        return pltpu.make_async_copy(band(b), w.at[OWN + b], load_sem.at[b])

    def load_old(b):
        return pltpu.make_async_copy(old.at[:, b], keep.at[b], old_sem.at[b])

    def store(b):
        return pltpu.make_async_copy(keep.at[b], out.at[:, b], out_sem.at[b])

    def die(i):
        return remote(band(2 * i + o), w.at[OTHER + i], die_s.at[i], die_r.at[i], base + o, gy)

    def across(b):
        h, j = (b % 4) // 2, b % 2
        at = (LEFT if b < 4 else RIGHT) + 2 * h + k
        return remote(
            band(b), w.at[at], row_s.at[b], row_r.at[at - LEFT],
            base + j, right if b < 4 else left,
        )

    def vertical(b):
        i, j = b // 2, b % 2
        at = LOWER - 4 * k + i
        chip = jnp.where(k == 0, above, below)
        return remote(band(b), w.at[at], col_s.at[b], col_r.at[at - UPPER], chip + j, gy)

    def return_p(h, i):
        return remote(
            sent_p.at[h, i], got_p.at[2 * h + k], p_s.at[h, i], p_r.at[2 * h + k],
            base + i, left,
        )

    def return_q(h, i):
        row = above + 1 if i == 0 else below
        return remote(
            sent_q.at[h, i], got_q.at[2 * h + k], q_s.at[h, i], q_r.at[2 * h + k], row, gy
        )

    def hand_e(i, b):
        return remote(
            cross.at[1, b, 1], cross.at[0, b, 1], e_s.at[i], e_r.at[i], base + o, gy
        )

    def hand_d(h, b, owner):
        part = pl.ds(3 - owner, 2)
        return remote(
            cross.at[1, b, part], cross.at[0, b, part], d_s.at[h], d_r.at[h], base + o, gy
        )

    def arrival(dst, sem):
        return remote(dst, dst, load_sem.at[0], sem, base + o, gy)

    barrier = pltpu.get_barrier_semaphore()
    greeted = [
        (base, left), (base + 1, left), (base, right), (base + 1, right), (base + o, gy),
        (jnp.where(k == 0, above, below), gy), (jnp.where(k == 0, above, below) + 1, gy),
        (jnp.where(k == 0, below, above + 1), gy),
    ]
    for where in greeted:
        pl.semaphore_signal(barrier, inc=1, device_id=where, device_id_type=MESH)

    def start_load(b, carry):
        load(b).start()
        return carry

    lax.fori_loop(0, BANDS, start_load, 0)
    pl.semaphore_wait(barrier, len(greeted))

    for b in range(4):
        across(b).start()
        across(4 + b).start()
    for b in (0, 4, 1, 5, 2, 6, 3, 7):
        vertical(b).start()
    for i in (0, 2, 1, 3):
        die(i).start()

    def start_old(b, carry):
        load_old(b).start()
        return carry

    lax.fori_loop(0, BANDS, start_old, 0)

    lane = lax.broadcasted_iota(jnp.int32, (ST, ST), 1)
    word = lane // 30
    shift = lane - word * 30
    for s in range(SLOTS):
        chosen = jnp.zeros((ST, ST), jnp.int32)
        for n in range(WORDS):
            chosen = jnp.where(word == n, bits[s, :, n:n + 1], chosen)
        mask[s] = (lax.shift_right_logical(chosen, shift) & 1).astype(jnp.float32)
    pick[0] = jnp.zeros((2 * ST, ST), jnp.float32)

    def own_band(b, carry):
        load(b).wait()
        whiten(w, OWN + b)
        real, imag = pair(w, OWN + b, OWN + b)
        cross[0, b, 0, :ST, :] = real
        cross[0, b, 0, ST:, :] = imag
        return carry

    lax.fori_loop(0, BANDS, own_band, 0)

    def chip_block(a, i):
        return jnp.where(a == k, OWN + 2 * i + k, OTHER + i)

    def put(owner, b, code, value):
        side = jnp.where(owner == k, 0, 1)
        cross[side, b, code, :ST, :] = value[0]
        cross[side, b, code, ST:, :] = value[1]

    def common(i):
        b = 2 * i + k
        arrival(w.at[OTHER + i], die_r.at[i]).wait_recv()
        arrival(w.at[UPPER + i], col_r.at[i]).wait_recv()
        arrival(w.at[LOWER + i], col_r.at[4 + i]).wait_recv()

        def whiten_one(n, carry):
            whiten(w, OTHER + 4 * n + i)
            return carry

        lax.fori_loop(0, 3, whiten_one, 0)

        def below_pair(a, carry):
            x = chip_block(a, i)
            y = jnp.where(a == 0, chip_block(1, i), LOWER + i)
            put(a, b, 1, pair(w, x, y))
            return carry

        lax.fori_loop(0, 2, below_pair, 0)

    def stage(h, carry):
        i = h
        b = 2 * i + k
        common(i)
        for n in range(2):
            arrival(w.at[LEFT + 2 * h + n], row_r.at[2 * h + n]).wait_recv()
        hand_e(i, b).start()
        for n in range(2):
            whiten(w, LEFT + 2 * h + n)

        def left_pair(n, carry):
            own, a = n // 2, n % 2
            real, imag = pair(w, LEFT + 2 * h + own, chip_block(a, i))
            sent_p[h, own, 1 + a - own, :ST, :] = real.astype(jnp.bfloat16)
            sent_p[h, own, 1 + a - own, ST:, :] = imag.astype(jnp.bfloat16)
            return carry

        lax.fori_loop(0, 4, left_pair, 0)

        def left_corner(own, carry):
            real, imag = pair(w, LEFT + 2 * h + own, UPPER + 4 * own + i)
            sent_p[h, own, 2 * own, :ST, :] = real.astype(jnp.bfloat16)
            sent_p[h, own, 2 * own, ST:, :] = imag.astype(jnp.bfloat16)
            return carry

        lax.fori_loop(0, 2, left_corner, 0)

        i = 2 + h
        b = 2 * i + k
        common(i)
        for n in range(2):
            return_p(h, n).start()
        for n in range(2):
            arrival(w.at[RIGHT + 2 * h + n], row_r.at[4 + 2 * h + n]).wait_recv()
        hand_e(i, b).start()
        for n in range(2):
            whiten(w, RIGHT + 2 * h + n)

        def right_corner(n, carry):
            real, imag = pair(w, UPPER + 4 * n + i, RIGHT + 2 * h + n)
            sent_q[h, n, :ST, :] = real.astype(jnp.bfloat16)
            sent_q[h, n, ST:, :] = imag.astype(jnp.bfloat16)
            return carry

        lax.fori_loop(0, 2, right_corner, 0)

        def right_pair(n, carry):
            a, far = n // 2, n % 2
            put(a, b, 3 + far - a, pair(w, chip_block(a, i), RIGHT + 2 * h + far))
            return carry

        lax.fori_loop(0, 4, right_pair, 0)
        for n in range(2):
            return_q(h, n).start()
        hand_d(h, b, o).start()
        return carry

    lax.fori_loop(0, 2, stage, 0)

    def combine(b):
        load_old(b).wait()
        for s in range(SLOTS):
            which = codes[s] + 1
            flags = mask[s]
            keep[b, s, :ST, :] = keep[b, s, :ST, :] + flags * pick[which, :ST, :]
            keep[b, s, ST:, :] = keep[b, s, ST:, :] + flags * pick[which, ST:, :]
        store(b).start()

    def finish_q(n, carry):
        b = 4 + n
        i, j = b // 2, lax.rem(b, 2)
        h = n // 2

        @pl.when(j == o)
        def _():
            arrival(cross.at[0, b, 1], e_r.at[i]).wait_recv()
            part = pl.ds(3 - k, 2)
            arrival(cross.at[0, b, part], d_r.at[h]).wait_recv()

        arrival(got_q.at[n], q_r.at[n]).wait_recv()
        pick[1] = cross[0, b, 0]
        pick[2] = cross[0, b, 1]
        pick[4] = cross[0, b, 3]
        pick[pl.ds(3 + 2 * o, 1)] = cross[0, b, pl.ds(2 + 2 * o, 1)]
        pick[pl.ds(3 + 2 * k, 1)] = got_q[pl.ds(n, 1)].astype(jnp.float32)
        combine(b)
        return carry

    lax.fori_loop(0, 4, finish_q, 0)

    def finish_p(b, carry):
        i, j = b // 2, lax.rem(b, 2)

        @pl.when(j == o)
        def _():
            arrival(cross.at[0, b, 1], e_r.at[i]).wait_recv()

        arrival(got_p.at[b], p_r.at[b]).wait_recv()
        pick[1] = cross[0, b, 0]
        pick[2] = cross[0, b, 1]
        for n in range(3):
            pick[3 + n] = got_p[b, n].astype(jnp.float32)
        combine(b)
        return carry

    lax.fori_loop(0, 4, finish_p, 0)

    for b in range(BANDS):
        across(b).wait_send()
        vertical(b).wait_send()
    for i in range(4):
        die(i).wait_send()
        hand_e(i, 2 * i + k).wait_send()
    for h in range(2):
        for n in range(2):
            return_p(h, n).wait_send()
            return_q(h, n).wait_send()
        hand_d(h, 4 + 2 * h + k, o).wait_send()
    for b in range(BANDS):
        store(b).wait()


def body(spectra, partner_codes, range_bits, old_stacks):
    codes = partner_codes.reshape(SLOTS)
    bits = range_bits.reshape(SLOTS, ST, WORDS)
    blocks = spectra.reshape(SEG, 2 * ST, BANDS * BW)
    old = old_stacks.reshape(SLOTS, BANDS, 2 * ST, ST)
    dma = pltpu.SemaphoreType.DMA
    updated = pl.pallas_call(
        kernel,
        out_shape=jax.ShapeDtypeStruct((SLOTS, BANDS, 2 * ST, ST), jnp.float32),
        in_specs=[
            pl.BlockSpec(memory_space=pltpu.SMEM),
            pl.BlockSpec(memory_space=pltpu.VMEM),
            pl.BlockSpec(memory_space=pl.ANY),
            pl.BlockSpec(memory_space=pl.ANY),
        ],
        out_specs=pl.BlockSpec(memory_space=pl.ANY),
        scratch_shapes=[
            pltpu.VMEM((PLACES, SEG, 2 * ST, BW), jnp.bfloat16),
            pltpu.VMEM((2, BANDS, SLOTS, 2 * ST, ST), jnp.float32),
            pltpu.VMEM((BANDS, SLOTS, 2 * ST, ST), jnp.float32),
            pltpu.VMEM((SLOTS, ST, ST), jnp.float32),
            pltpu.VMEM((SLOTS + 1, 2 * ST, ST), jnp.float32),
            pltpu.VMEM((2, 2, 3, 2 * ST, ST), jnp.bfloat16),
            pltpu.VMEM((4, 3, 2 * ST, ST), jnp.bfloat16),
            pltpu.VMEM((2, 2, 2 * ST, ST), jnp.bfloat16),
            pltpu.VMEM((4, 2 * ST, ST), jnp.bfloat16),
            dma((BANDS,)), dma((BANDS,)), dma((BANDS,)),
            dma((4,)), dma((4,)), dma((8,)), dma((8,)), dma((8,)), dma((8,)),
            dma((2, 2)), dma((4,)), dma((2, 2)), dma((4,)),
            dma((4,)), dma((4,)), dma((2,)), dma((2,)),
        ],
        compiler_params=pltpu.CompilerParams(
            collective_id=0, has_side_effects=True, vmem_limit_bytes=60 * 1024 * 1024
        ),
    )(codes, bits, blocks, old)
    return updated.reshape(old_stacks.shape)


def solution(mesh):
    return jax.shard_map(
        body,
        mesh=mesh,
        in_specs=(
            P("gx", "gy", None, None, None, None),
            P("gx", "gy", None),
            P("gx", "gy", None, None, None),
            P("gx", "gy", None, None, None, None, None),
        ),
        out_specs=P("gx", "gy", None, None, None, None, None),
        check_vma=False,
    )
```

profile of v0, /device:TPU:1, one launch (start us, length us, event | category | flops | bytes accessed | tf_op | source)
XLA Modules:
  0.0 103.9 jit_solution(6465046259715423137)
XLA Ops:
  0.0 1.6 %copy.5 = s32[1,1,5,128,5]{4,3,2,1,0:T(8,128)} copy(s32[1,1,5,128,5]{3,1,4,2,0:T(1,128)} %param.6) | data formatting | bytes 25600 | tf_op args[2]
  1.6 96.8 %shard_map.46 = f32[5,8,256,128]{3,2,1,0:T(8,128)} custom-call(s32[5]{0:T(128)} %bitcast.9, s32[5,128,5]{2,1,0:T(8,128)} %bitcast.8, bf16[3,256,4096]{2,1,0:T(8,128)(2,1)} %bitcast.6, f32[5,8,256,128]{3,2,1,0:T(8,128)} %bitcast.7), custom_call_target="tpu_custom_call" | custom-call | tf_op jit(solution)/shard_map/pallas_call | solution.py:340
  98.4 5.5 %copy.7 = f32[1,1,5,8,2,128,128]{6,5,4,3,2,1,0:T(8,128)} copy(f32[1,1,5,8,2,128,128]{6,5,4,3,2,1,0:T(8,128)} %bitcast.5) | data formatting | bytes 10485760
where the time goes:
time: 104 us
  Pallas kernels  96.8 us (93%)
  local copies, waits for them, and re-layouts  7.09 us (7%)
    pallas_call x1, Pallas kernels, body(): pl.pallas_call(kernel, out_shape=jax.ShapeDtypeStruct((SLOTS, BANDS, 2 *...  96.8 us
    unnamed x2, local copies, waits for them, and re-layouts  7.09 us

commit v1 on v0

--- a/solution.py
+++ b/solution.py
@@ -55,8 +55,8 @@
 
 def kernel(
     codes, bits, spectra, old, out,
-    w, cross, keep, mask, pick, sent_p, got_p, sent_q, got_q,
-    load_sem, old_sem, out_sem,
+    w, cross, mask, pick, sent_p, got_p, sent_q, got_q,
+    load_sem, old_sem,
     die_s, die_r, row_s, row_r, col_s, col_r,
     p_s, p_r, q_s, q_r, e_s, e_r, d_s, d_r,
 ):
@@ -83,10 +83,7 @@
         return pltpu.make_async_copy(band(b), w.at[OWN + b], load_sem.at[b])
 
     def load_old(b):
-        return pltpu.make_async_copy(old.at[:, b], keep.at[b], old_sem.at[b])
-
-    def store(b):
-        return pltpu.make_async_copy(keep.at[b], out.at[:, b], out_sem.at[b])
+        return pltpu.make_async_copy(old.at[:, b], out.at[:, b], old_sem.at[b])
 
     def die(i):
         return remote(band(2 * i + o), w.at[OTHER + i], die_s.at[i], die_r.at[i], base + o, gy)
@@ -161,14 +158,15 @@
 
     lax.fori_loop(0, BANDS, start_old, 0)
 
-    lane = lax.broadcasted_iota(jnp.int32, (ST, ST), 1)
-    word = lane // 30
-    shift = lane - word * 30
+    column = lax.broadcasted_iota(jnp.int32, (ST, ST), 0)
+    word = column // 30
+    shift = column - word * 30
     for s in range(SLOTS):
         chosen = jnp.zeros((ST, ST), jnp.int32)
         for n in range(WORDS):
-            chosen = jnp.where(word == n, bits[s, :, n:n + 1], chosen)
-        mask[s] = (lax.shift_right_logical(chosen, shift) & 1).astype(jnp.float32)
+            chosen = jnp.where(word == n, bits[s * WORDS + n], chosen)
+        flags = (lax.shift_right_logical(chosen, shift) & 1).astype(jnp.float32)
+        mask[s] = flags.T
     pick[0] = jnp.zeros((2 * ST, ST), jnp.float32)
 
     def own_band(b, carry):
@@ -273,9 +271,8 @@
         for s in range(SLOTS):
             which = codes[s] + 1
             flags = mask[s]
-            keep[b, s, :ST, :] = keep[b, s, :ST, :] + flags * pick[which, :ST, :]
-            keep[b, s, ST:, :] = keep[b, s, ST:, :] + flags * pick[which, ST:, :]
-        store(b).start()
+            out[s, b, :ST, :] = out[s, b, :ST, :] + flags * pick[which, :ST, :]
+            out[s, b, ST:, :] = out[s, b, ST:, :] + flags * pick[which, ST:, :]
 
     def finish_q(n, carry):
         b = 4 + n
@@ -327,43 +324,40 @@
             return_p(h, n).wait_send()
             return_q(h, n).wait_send()
         hand_d(h, 4 + 2 * h + k, o).wait_send()
-    for b in range(BANDS):
-        store(b).wait()
 
 
 def body(spectra, partner_codes, range_bits, old_stacks):
     codes = partner_codes.reshape(SLOTS)
-    bits = range_bits.reshape(SLOTS, ST, WORDS)
+    bits = jnp.swapaxes(range_bits.reshape(SLOTS, ST, WORDS), 1, 2).reshape(SLOTS * WORDS, 1, ST)
     blocks = spectra.reshape(SEG, 2 * ST, BANDS * BW)
     old = old_stacks.reshape(SLOTS, BANDS, 2 * ST, ST)
     dma = pltpu.SemaphoreType.DMA
     updated = pl.pallas_call(
         kernel,
-        out_shape=jax.ShapeDtypeStruct((SLOTS, BANDS, 2 * ST, ST), jnp.float32),
+        out_shape=pltpu.VMEM((SLOTS, BANDS, 2 * ST, ST), jnp.float32),
         in_specs=[
             pl.BlockSpec(memory_space=pltpu.SMEM),
             pl.BlockSpec(memory_space=pltpu.VMEM),
             pl.BlockSpec(memory_space=pl.ANY),
             pl.BlockSpec(memory_space=pl.ANY),
         ],
-        out_specs=pl.BlockSpec(memory_space=pl.ANY),
+        out_specs=pl.BlockSpec(memory_space=pltpu.VMEM),
         scratch_shapes=[
             pltpu.VMEM((PLACES, SEG, 2 * ST, BW), jnp.bfloat16),
             pltpu.VMEM((2, BANDS, SLOTS, 2 * ST, ST), jnp.float32),
-            pltpu.VMEM((BANDS, SLOTS, 2 * ST, ST), jnp.float32),
             pltpu.VMEM((SLOTS, ST, ST), jnp.float32),
             pltpu.VMEM((SLOTS + 1, 2 * ST, ST), jnp.float32),
             pltpu.VMEM((2, 2, 3, 2 * ST, ST), jnp.bfloat16),
             pltpu.VMEM((4, 3, 2 * ST, ST), jnp.bfloat16),
             pltpu.VMEM((2, 2, 2 * ST, ST), jnp.bfloat16),
             pltpu.VMEM((4, 2 * ST, ST), jnp.bfloat16),
-            dma((BANDS,)), dma((BANDS,)), dma((BANDS,)),
+            dma((BANDS,)), dma((BANDS,)),
             dma((4,)), dma((4,)), dma((8,)), dma((8,)), dma((8,)), dma((8,)),
             dma((2, 2)), dma((4,)), dma((2, 2)), dma((4,)),
             dma((4,)), dma((4,)), dma((2,)), dma((2,)),
         ],
         compiler_params=pltpu.CompilerParams(
-            collective_id=0, has_side_effects=True, vmem_limit_bytes=60 * 1024 * 1024
+            collective_id=0, has_side_effects=True, vmem_limit_bytes=52 * 1024 * 1024
         ),
     )(codes, bits, blocks, old)
     return updated.reshape(old_stacks.shape)

time: 104 us -> 99.3 us (0.955)
  local copies, waits for them, and re-layouts: 7.09 us -> 3.69 us
  Pallas kernels: 96.8 us -> 95.4 us
    unnamed x2, local copies, waits for them, and re-layouts: 7.09 us -> 3.07 us
    pallas_call x1, Pallas kernels: 96.8 us -> 95.4 us  [body(): pl.pallas_call(kernel, out_shape=pltpu.VMEM((SLOTS, BANDS, 2 * ST, ST), j...]
where the time goes in v1:
time: 99.3 us; the launch traced here: 99.1 us
  Pallas kernels  95.4 us (96%)
  local copies, waits for them, and re-layouts  3.69 us (4%)
    pallas_call x1, Pallas kernels, body(): pl.pallas_call(kernel, out_shape=pltpu.VMEM((SLOTS, BANDS, 2 * ST, ST), j...  95.4 us
    unnamed x2, local copies, waits for them, and re-layouts  3.07 us

profile of v1, /device:TPU:1, one launch (start us, length us, event | category | flops | bytes accessed | tf_op | source)
XLA Modules:
  0.0 99.1 jit_solution(15018427217271416686)
XLA Ops:
  0.0 0.7 copy.7
  0.7 0.6 reshape.20.bits
  1.3 95.4 %shard_map.46 = f32[5,8,256,128]{3,2,1,0:T(8,128)S(1)} custom-call(s32[5]{0:T(128)} %bitcast.13, s32[25,1,128]{2,1,0:T(1,128)} %reshape.20.bits, bf16[3,256,4096]{2,1,0:T(8,128)(2,1)} %bitcast.10, f32[5,8,256,128]{3,2,1,0:T(8,128)} %bitcast.11), custom_call_target="tpu_custom_call" | custom-call | tf_op jit(solution)/shard_map/pallas_call | solution.py:335
  96.7 2.4 %copy.9 = f32[1,1,5,8,2,128,128]{6,5,4,3,2,1,0:T(8,128)} copy(f32[1,1,5,8,2,128,128]{6,5,4,3,2,1,0:T(8,128)S(1)} %bitcast.9) | data formatting | bytes 10485760

commit v2 on v1

--- a/solution.py
+++ b/solution.py
@@ -328,7 +328,7 @@
 
 def body(spectra, partner_codes, range_bits, old_stacks):
     codes = partner_codes.reshape(SLOTS)
-    bits = jnp.swapaxes(range_bits.reshape(SLOTS, ST, WORDS), 1, 2).reshape(SLOTS * WORDS, 1, ST)
+    bits = jnp.transpose(range_bits, (0, 2, 4, 1, 3)).reshape(SLOTS * WORDS, 1, ST)
     blocks = spectra.reshape(SEG, 2 * ST, BANDS * BW)
     old = old_stacks.reshape(SLOTS, BANDS, 2 * ST, ST)
     dma = pltpu.SemaphoreType.DMA

time: 99.3 us -> 97.9 us (0.986)
  local copies, waits for them, and re-layouts: 3.69 us -> 2.36 us
    unnamed x2 -> x1, local copies, waits for them, and re-layouts: 3.07 us -> 2.36 us
where the time goes in v2:
time: 97.9 us; the launch traced here: 97.7 us
  Pallas kernels  95.3 us (97%)
  local copies, waits for them, and re-layouts  2.36 us (2%)
    pallas_call x1, Pallas kernels, body(): pl.pallas_call(kernel, out_shape=pltpu.VMEM((SLOTS, BANDS, 2 * ST, ST), j...  95.3 us
    unnamed x1, local copies, waits for them, and re-layouts  2.36 us

profile of v2, /device:TPU:1, one launch (start us, length us, event | category | flops | bytes accessed | tf_op | source)
XLA Modules:
  0.0 97.7 jit_solution(4117433546256385611)
XLA Ops:
  0.0 95.3 %shard_map.46 = f32[5,8,256,128]{3,2,1,0:T(8,128)S(1)} custom-call(s32[5]{0:T(128)} %bitcast.11, s32[25,1,128]{2,1,0:T(1,128)} %bitcast.10, bf16[3,256,4096]{2,1,0:T(8,128)(2,1)} %bitcast.8, f32[5,8,256,128]{3,2,1,0:T(8,128)} %bitcast.9), custom_call_target="tpu_custom_call" | custom-call | tf_op jit(solution)/shard_map/pallas_call | solution.py:335
  95.3 2.4 %copy.6 = f32[1,1,5,8,2,128,128]{6,5,4,3,2,1,0:T(8,128)} copy(f32[1,1,5,8,2,128,128]{6,5,4,3,2,1,0:T(8,128)S(1)} %bitcast.7) | data formatting | bytes 10485760

commit v3 on v2

--- a/solution.py
+++ b/solution.py
@@ -69,6 +69,10 @@
     left = lax.rem(gy + COLS - 1, COLS)
     above = lax.rem(base + ROWS - 2, ROWS)
     below = lax.rem(base + 2, ROWS)
+    has_left, has_right = gy > 0, gy < COLS - 1
+    has_above, has_below = base > 0, base < ROWS - 2
+    swaps = jnp.where(k == 0, base > 0, base < ROWS - 2)
+    hears = jnp.where(k == 0, base < ROWS - 2, base > 0)
 
     def band(b):
         return spectra.at[:, :, pl.ds(pl.multiple_of(b * BW, BW), BW)]
@@ -129,26 +133,45 @@
         return remote(dst, dst, load_sem.at[0], sem, base + o, gy)
 
     barrier = pltpu.get_barrier_semaphore()
-    greeted = [
-        (base, left), (base + 1, left), (base, right), (base + 1, right), (base + o, gy),
-        (jnp.where(k == 0, above, below), gy), (jnp.where(k == 0, above, below) + 1, gy),
-        (jnp.where(k == 0, below, above + 1), gy),
-    ]
-    for where in greeted:
-        pl.semaphore_signal(barrier, inc=1, device_id=where, device_id_type=MESH)
+    def greet(there, row, col):
+        @pl.when(there)
+        def _():
+            pl.semaphore_signal(barrier, inc=1, device_id=(row, col), device_id_type=MESH)
+
+    chip = jnp.where(k == 0, above, below)
+    pl.semaphore_signal(barrier, inc=1, device_id=(base + o, gy), device_id_type=MESH)
+    for n in range(2):
+        greet(swaps, chip + n, gy)
+        greet(has_left, base + n, left)
+        greet(has_right, base + n, right)
+    greet(hears, jnp.where(k == 0, below, above + 1), gy)
+    partners = (
+        1 + hears.astype(jnp.int32)
+        + 2 * (swaps.astype(jnp.int32) + has_left.astype(jnp.int32) + has_right.astype(jnp.int32))
+    )
 
     def start_load(b, carry):
         load(b).start()
         return carry
 
     lax.fori_loop(0, BANDS, start_load, 0)
-    pl.semaphore_wait(barrier, len(greeted))
-
-    for b in range(4):
-        across(b).start()
-        across(4 + b).start()
-    for b in (0, 4, 1, 5, 2, 6, 3, 7):
-        vertical(b).start()
+    pl.semaphore_wait(barrier, partners)
+
+    @pl.when(has_right)
+    def _():
+        for b in range(4):
+            across(b).start()
+
+    @pl.when(has_left)
+    def _():
+        for b in range(4):
+            across(4 + b).start()
+
+    @pl.when(swaps)
+    def _():
+        for b in (0, 4, 1, 5, 2, 6, 3, 7):
+            vertical(b).start()
+
     for i in (0, 2, 1, 3):
         die(i).start()
 
@@ -190,8 +213,14 @@
     def common(i):
         b = 2 * i + k
         arrival(w.at[OTHER + i], die_r.at[i]).wait_recv()
-        arrival(w.at[UPPER + i], col_r.at[i]).wait_recv()
-        arrival(w.at[LOWER + i], col_r.at[4 + i]).wait_recv()
+
+        @pl.when(has_above)
+        def _():
+            arrival(w.at[UPPER + i], col_r.at[i]).wait_recv()
+
+        @pl.when(has_below)
+        def _():
+            arrival(w.at[LOWER + i], col_r.at[4 + i]).wait_recv()
 
         def whiten_one(n, carry):
             whiten(w, OTHER + 4 * n + i)
@@ -207,13 +236,9 @@
 
         lax.fori_loop(0, 2, below_pair, 0)
 
-    def stage(h, carry):
-        i = h
-        b = 2 * i + k
-        common(i)
+    def from_left(h, i):
         for n in range(2):
             arrival(w.at[LEFT + 2 * h + n], row_r.at[2 * h + n]).wait_recv()
-        hand_e(i, b).start()
         for n in range(2):
             whiten(w, LEFT + 2 * h + n)
 
@@ -234,14 +259,9 @@
 
         lax.fori_loop(0, 2, left_corner, 0)
 
-        i = 2 + h
-        b = 2 * i + k
-        common(i)
-        for n in range(2):
-            return_p(h, n).start()
+    def from_right(h, i, b):
         for n in range(2):
             arrival(w.at[RIGHT + 2 * h + n], row_r.at[4 + 2 * h + n]).wait_recv()
-        hand_e(i, b).start()
         for n in range(2):
             whiten(w, RIGHT + 2 * h + n)
 
@@ -259,9 +279,38 @@
             return carry
 
         lax.fori_loop(0, 4, right_pair, 0)
-        for n in range(2):
-            return_q(h, n).start()
+
+        @pl.when(has_above)
+        def _():
+            return_q(h, 0).start()
+
+        @pl.when(has_below)
+        def _():
+            return_q(h, 1).start()
+
         hand_d(h, b, o).start()
+
+    def stage(h, carry):
+        common(h)
+
+        @pl.when(has_left)
+        def _():
+            from_left(h, h)
+
+        hand_e(h, 2 * h + k).start()
+        i = 2 + h
+        common(i)
+
+        @pl.when(has_left)
+        def _():
+            for n in range(2):
+                return_p(h, n).start()
+
+        @pl.when(has_right)
+        def _():
+            from_right(h, i, 2 * i + k)
+
+        hand_e(i, 2 * i + k).start()
         return carry
 
     lax.fori_loop(0, 2, stage, 0)
@@ -282,10 +331,16 @@
         @pl.when(j == o)
         def _():
             arrival(cross.at[0, b, 1], e_r.at[i]).wait_recv()
+
+        @pl.when((j == o) & has_right)
+        def _():
             part = pl.ds(3 - k, 2)
             arrival(cross.at[0, b, part], d_r.at[h]).wait_recv()
 
-        arrival(got_q.at[n], q_r.at[n]).wait_recv()
+        @pl.when(swaps & has_right)
+        def _():
+            arrival(got_q.at[n], q_r.at[n]).wait_recv()
+
         pick[1] = cross[0, b, 0]
         pick[2] = cross[0, b, 1]
         pick[4] = cross[0, b, 3]
@@ -303,7 +358,10 @@
         def _():
             arrival(cross.at[0, b, 1], e_r.at[i]).wait_recv()
 
-        arrival(got_p.at[b], p_r.at[b]).wait_recv()
+        @pl.when(has_right)
+        def _():
+            arrival(got_p.at[b], p_r.at[b]).wait_recv()
+
         pick[1] = cross[0, b, 0]
         pick[2] = cross[0, b, 1]
         for n in range(3):
@@ -313,17 +371,39 @@
 
     lax.fori_loop(0, 4, finish_p, 0)
 
-    for b in range(BANDS):
-        across(b).wait_send()
-        vertical(b).wait_send()
     for i in range(4):
         die(i).wait_send()
         hand_e(i, 2 * i + k).wait_send()
+
+    @pl.when(swaps)
+    def _():
+        for b in range(BANDS):
+            vertical(b).wait_send()
+
+    @pl.when(has_left)
+    def _():
+        for b in range(4):
+            across(4 + b).wait_send()
+        for h in range(2):
+            for n in range(2):
+                return_p(h, n).wait_send()
+
+    @pl.when(has_right)
+    def _():
+        for b in range(4):
+            across(b).wait_send()
+        for h in range(2):
+            hand_d(h, 4 + 2 * h + k, o).wait_send()
+
     for h in range(2):
-        for n in range(2):
-            return_p(h, n).wait_send()
-            return_q(h, n).wait_send()
-        hand_d(h, 4 + 2 * h + k, o).wait_send()
+
+        @pl.when(has_right & has_above)
+        def _():
+            return_q(h, 0).wait_send()
+
+        @pl.when(has_right & has_below)
+        def _():
+            return_q(h, 1).wait_send()
 
 
 def body(spectra, partner_codes, range_bits, old_stacks):

time: 97.9 us -> 93.8 us (0.958)
  Pallas kernels: 95.3 us -> 91 us
    pallas_call x1, Pallas kernels: 95.3 us -> 91 us  [body(): pl.pallas_call(kernel, out_shape=pltpu.VMEM((SLOTS, BANDS, 2 * ST, ST), j...]
where the time goes in v3:
time: 93.8 us; the launch traced here: 93.4 us
  Pallas kernels  91 us (97%)
  local copies, waits for them, and re-layouts  2.36 us (3%)
    pallas_call x1, Pallas kernels, body(): pl.pallas_call(kernel, out_shape=pltpu.VMEM((SLOTS, BANDS, 2 * ST, ST), j...  91 us
    unnamed x1, local copies, waits for them, and re-layouts  2.36 us

profile of v3, /device:TPU:1, one launch (start us, length us, event | category | flops | bytes accessed | tf_op | source)
XLA Modules:
  0.0 93.4 jit_solution(14089884740937409875)
XLA Ops:
  0.0 91.0 %shard_map.46 = f32[5,8,256,128]{3,2,1,0:T(8,128)S(1)} custom-call(s32[5]{0:T(128)} %bitcast.11, s32[25,1,128]{2,1,0:T(1,128)} %bitcast.10, bf16[3,256,4096]{2,1,0:T(8,128)(2,1)} %bitcast.8, f32[5,8,256,128]{3,2,1,0:T(8,128)} %bitcast.9), custom_call_target="tpu_custom_call" | custom-call | tf_op jit(solution)/shard_map/pallas_call | solution.py:415
  91.0 2.4 %copy.6 = f32[1,1,5,8,2,128,128]{6,5,4,3,2,1,0:T(8,128)} copy(f32[1,1,5,8,2,128,128]{6,5,4,3,2,1,0:T(8,128)S(1)} %bitcast.7) | data formatting | bytes 10485760

commit v4 on v3

--- a/solution.py
+++ b/solution.py
@@ -19,46 +19,56 @@
 WORDS = 5
 SCALE = 1.0 / math.sqrt(SEG * BW)
 
-OWN, OTHER, UPPER, LOWER, LEFT, RIGHT, PLACES = 0, 8, 12, 16, 20, 24, 28
+OWN, OTHER, UPPER, LOWER, LEFT, RIGHT, HALF, PLACES = 0, 8, 12, 16, 20, 24, 28, 30
+CUT = 4
+HB = BW // 2
+HR = ST // 2
 
 
 def whiten(w, place):
     def rows_of(t, carry):
-        first = pl.multiple_of(t * 16, 16)
+        rows = pl.ds(pl.multiple_of(t * 16, 16), 16)
         total = jnp.zeros((16, BW), jnp.float32)
         for s in range(SEG):
             for c in range(2):
-                x = w[place, s, pl.ds(c * ST + first, 16), :].astype(jnp.float32)
+                x = w[place, s, c, rows, :].astype(jnp.float32)
                 total = total + x * x
         power = jnp.sum(total, axis=-1, keepdims=True) * (1.0 / (SEG * 2 * BW))
         gain = lax.rsqrt(power + EPSILON)
         for s in range(SEG):
             for c in range(2):
-                x = w[place, s, pl.ds(c * ST + first, 16), :].astype(jnp.float32)
-                w[place, s, pl.ds(c * ST + first, 16), :] = (x * gain).astype(jnp.bfloat16)
+                x = w[place, s, c, rows, :].astype(jnp.float32)
+                w[place, s, c, rows, :] = (x * gain).astype(jnp.bfloat16)
         return carry
 
-    lax.fori_loop(0, ST // 16, rows_of, 0)
-
-
-def pair(w, x, y):
+    lax.fori_loop(0, ST // 16, rows_of, 0, unroll=4)
+
+
+def pair(w, x, y, first=0, rows=ST, bins=BW):
     total = None
     for s in range(SEG):
         part = lax.dot_general(
-            w[x, s], w[y, s], (((1,), (1,)), ((), ())), preferred_element_type=jnp.float32
+            w[x, s, :, first:first + rows, :bins].reshape(2 * rows, bins),
+            w[y, s, :, :, :bins].reshape(2 * ST, bins),
+            (((1,), (1,)), ((), ())), preferred_element_type=jnp.float32,
         )
         total = part if total is None else total + part
-    real = (total[:ST, :ST] + total[ST:, ST:]) * SCALE
-    imag = (total[ST:, :ST] - total[:ST, ST:]) * SCALE
+    real = (total[:rows, :ST] + total[rows:, ST:]) * SCALE
+    imag = (total[rows:, :ST] - total[:rows, ST:]) * SCALE
     return real, imag
+
+
+def turn(h, core):
+    return jnp.where(h == 0, 6 - core, CUT + 3 * core)
 
 
 def kernel(
     codes, bits, spectra, old, out,
-    w, cross, mask, pick, sent_p, got_p, sent_q, got_q,
+    w, cross, mask, pick, sent_p, got_p, sent_q, got_q, sent_m, got_m,
     load_sem, old_sem,
     die_s, die_r, row_s, row_r, col_s, col_r,
     p_s, p_r, q_s, q_r, e_s, e_r, d_s, d_r,
+    half_s, half_r, m_s, m_r, ready_right, ready_below,
 ):
     gx = lax.axis_index("gx")
     gy = lax.axis_index("gy")
@@ -75,7 +85,7 @@
     hears = jnp.where(k == 0, base < ROWS - 2, base > 0)
 
     def band(b):
-        return spectra.at[:, :, pl.ds(pl.multiple_of(b * BW, BW), BW)]
+        return spectra.at[:, :, :, pl.ds(pl.multiple_of(b * BW, BW), BW)]
 
     def remote(src, dst, send, recv, row, col):
         return pltpu.make_async_remote_copy(
@@ -93,11 +103,32 @@
         return remote(band(2 * i + o), w.at[OTHER + i], die_s.at[i], die_r.at[i], base + o, gy)
 
     def across(b):
-        h, j = (b % 4) // 2, b % 2
-        at = (LEFT if b < 4 else RIGHT) + 2 * h + k
+        if b == CUT:
+            part = pl.ds(HB, HB)
+            at = RIGHT + 2 + k
+            return remote(
+                w.at[OWN + CUT, :, :, :, part], w.at[at, :, :, :, part],
+                row_s.at[b], row_r.at[at - LEFT], base, left,
+            )
+        h, j = {0: 0, 1: 0, 2: 1, 3: 1, 6: 0, 5: 0, 7: 1}[b], b % 2
+        at = (LEFT if b < CUT else RIGHT) + 2 * h + k
         return remote(
             band(b), w.at[at], row_s.at[b], row_r.at[at - LEFT],
-            base + j, right if b < 4 else left,
+            base + j, right if b < CUT else left,
+        )
+
+    def half(c):
+        rows, part = pl.ds(c * HR, HR), pl.ds(0, HB)
+        return remote(
+            w.at[OWN + CUT, :, :, rows, part], w.at[HALF + k, :, :, rows, part],
+            half_s.at[c], half_r.at[c, k], base, right,
+        )
+
+    def return_m(c, i):
+        rows = pl.ds(c * HR, HR)
+        return remote(
+            sent_m.at[i, :, :, rows], got_m.at[:, :, rows], m_s.at[c, i], m_r.at[c],
+            base + i, left,
         )
 
     def vertical(b):
@@ -133,47 +164,61 @@
         return remote(dst, dst, load_sem.at[0], sem, base + o, gy)
 
     barrier = pltpu.get_barrier_semaphore()
-    def greet(there, row, col):
+
+    def greet(there, sem, row, col):
         @pl.when(there)
         def _():
-            pl.semaphore_signal(barrier, inc=1, device_id=(row, col), device_id_type=MESH)
-
-    chip = jnp.where(k == 0, above, below)
+            pl.semaphore_signal(sem, inc=1, device_id=(row, col), device_id_type=MESH)
+
+    def count(there):
+        return there.astype(jnp.int32)
+
     pl.semaphore_signal(barrier, inc=1, device_id=(base + o, gy), device_id_type=MESH)
     for n in range(2):
-        greet(swaps, chip + n, gy)
-        greet(has_left, base + n, left)
-        greet(has_right, base + n, right)
-    greet(hears, jnp.where(k == 0, below, above + 1), gy)
-    partners = (
-        1 + hears.astype(jnp.int32)
-        + 2 * (swaps.astype(jnp.int32) + has_left.astype(jnp.int32) + has_right.astype(jnp.int32))
-    )
+        greet(has_right, barrier, base + n, right)
+    greet(has_below, barrier, below, gy)
+    greet(has_below & (k == 1), barrier, below + 1, gy)
 
     def start_load(b, carry):
-        load(b).start()
+        load(lax.rem(b + CUT, BANDS)).start()
         return carry
 
     lax.fori_loop(0, BANDS, start_load, 0)
-    pl.semaphore_wait(barrier, partners)
+    pl.semaphore_wait(barrier, 1 + 2 * count(has_left) + (2 - k) * count(has_above))
+    for n in range(2):
+        greet(has_left, ready_right, base + n, left)
+    greet(has_above, ready_below, above + 1, gy)
+    greet(has_above & (k == 0), ready_below, above, gy)
+
+    vertical_order = (0, 5, 1, 7, 2, 6, 4, 3)
+
+    @pl.when(has_left)
+    def _():
+        for b in (5, 7, 6):
+            across(b).start()
+
+    @pl.when(has_above & (k == 0))
+    def _():
+        for b in vertical_order:
+            vertical(b).start()
+
+    for i in (0, 3, 2, 1):
+        die(i).start()
 
     @pl.when(has_right)
     def _():
+        pl.semaphore_wait(ready_right, 2)
         for b in range(4):
             across(b).start()
 
-    @pl.when(has_left)
-    def _():
-        for b in range(4):
-            across(4 + b).start()
-
-    @pl.when(swaps)
-    def _():
-        for b in (0, 4, 1, 5, 2, 6, 3, 7):
+    @pl.when(has_below)
+    def _():
+        pl.semaphore_wait(ready_below, 1 + k)
+
+    @pl.when(has_below & (k == 1))
+    def _():
+        for b in vertical_order:
             vertical(b).start()
-
-    for i in (0, 2, 1, 3):
-        die(i).start()
 
     def start_old(b, carry):
         load_old(b).start()
@@ -192,9 +237,22 @@
         mask[s] = flags.T
     pick[0] = jnp.zeros((2 * ST, ST), jnp.float32)
 
-    def own_band(b, carry):
+    def own_band(n, carry):
+        b = lax.rem(n + CUT, BANDS)
         load(b).wait()
         whiten(w, OWN + b)
+
+        @pl.when(n == 1)
+        def _():
+            @pl.when(has_left)
+            def _():
+                across(CUT).start()
+
+            @pl.when(has_right)
+            def _():
+                for c in range(2):
+                    half(c).start()
+
         real, imag = pair(w, OWN + b, OWN + b)
         cross[0, b, 0, :ST, :] = real
         cross[0, b, 0, ST:, :] = imag
@@ -202,6 +260,11 @@
 
     lax.fori_loop(0, BANDS, own_band, 0)
 
+    @pl.when(k == 0)
+    def _():
+        for n in range(2):
+            w[RIGHT + 2 + n, :, :, :, :HB] = jnp.zeros((SEG, 2, ST, HB), jnp.bfloat16)
+
     def chip_block(a, i):
         return jnp.where(a == k, OWN + 2 * i + k, OTHER + i)
 
@@ -211,7 +274,6 @@
         cross[side, b, code, ST:, :] = value[1]
 
     def common(i):
-        b = 2 * i + k
         arrival(w.at[OTHER + i], die_r.at[i]).wait_recv()
 
         @pl.when(has_above)
@@ -228,10 +290,18 @@
 
         lax.fori_loop(0, 3, whiten_one, 0)
 
+    def whiten_two(place):
+        def whiten_one(n, carry):
+            whiten(w, place + n)
+            return carry
+
+        lax.fori_loop(0, 2, whiten_one, 0)
+
+    def own_column(i):
         def below_pair(a, carry):
             x = chip_block(a, i)
             y = jnp.where(a == 0, chip_block(1, i), LOWER + i)
-            put(a, b, 1, pair(w, x, y))
+            put(a, 2 * i + k, 1, pair(w, x, y))
             return carry
 
         lax.fori_loop(0, 2, below_pair, 0)
@@ -239,8 +309,7 @@
     def from_left(h, i):
         for n in range(2):
             arrival(w.at[LEFT + 2 * h + n], row_r.at[2 * h + n]).wait_recv()
-        for n in range(2):
-            whiten(w, LEFT + 2 * h + n)
+        whiten_two(LEFT + 2 * h)
 
         def left_pair(n, carry):
             own, a = n // 2, n % 2
@@ -260,10 +329,19 @@
         lax.fori_loop(0, 2, left_corner, 0)
 
     def from_right(h, i, b):
-        for n in range(2):
-            arrival(w.at[RIGHT + 2 * h + n], row_r.at[4 + 2 * h + n]).wait_recv()
-        for n in range(2):
-            whiten(w, RIGHT + 2 * h + n)
+        cut = (h == 1) & (k == 0)
+
+        @pl.when(cut)
+        def _():
+            for n in range(2):
+                part = w.at[RIGHT + 2 + n, :, :, :, pl.ds(HB, HB)]
+                arrival(part, row_r.at[6 + n]).wait_recv()
+
+        @pl.when(jnp.logical_not(cut))
+        def _():
+            for n in range(2):
+                arrival(w.at[RIGHT + 2 * h + n], row_r.at[4 + 2 * h + n]).wait_recv()
+            whiten_two(RIGHT + 2 * h)
 
         def right_corner(n, carry):
             real, imag = pair(w, UPPER + 4 * n + i, RIGHT + 2 * h + n)
@@ -297,23 +375,51 @@
         def _():
             from_left(h, h)
 
-        hand_e(h, 2 * h + k).start()
-        i = 2 + h
-        common(i)
+        own_column(h)
 
         @pl.when(has_left)
         def _():
             for n in range(2):
                 return_p(h, n).start()
 
+        b = turn(h, k)
+        i = b // 2
+        hand_e(h, 2 * h + k).start()
+        common(i)
+        own_column(i)
+
         @pl.when(has_right)
         def _():
-            from_right(h, i, 2 * i + k)
-
-        hand_e(i, 2 * i + k).start()
+            from_right(h, i, b)
+
+        hand_e(i, b).start()
         return carry
 
     lax.fori_loop(0, 2, stage, 0)
+
+    def half_products(c):
+        i = CUT // 2
+        for n in range(2):
+            part = w.at[HALF + n, :, :, pl.ds(c * HR, HR), pl.ds(0, HB)]
+            arrival(part, half_r.at[c, n]).wait_recv()
+
+        def half_put(own, code, y):
+            real, imag = pair(w, HALF + own, y, c * HR, HR, HB)
+            sent_m[own, code, 0, c * HR:(c + 1) * HR, :] = real.astype(jnp.bfloat16)
+            sent_m[own, code, 1, c * HR:(c + 1) * HR, :] = imag.astype(jnp.bfloat16)
+
+        def half_pair(n, carry):
+            own, a = n // 2, n % 2
+            half_put(own, 1 + a - own, chip_block(a, i))
+            return carry
+
+        lax.fori_loop(0, 4, half_pair, 0)
+
+        def half_corner(own, carry):
+            half_put(own, 2 * own, UPPER + 4 * own + i)
+            return carry
+
+        lax.fori_loop(0, 2, half_corner, 0)
 
     def combine(b):
         load_old(b).wait()
@@ -323,33 +429,45 @@
             out[s, b, :ST, :] = out[s, b, :ST, :] + flags * pick[which, :ST, :]
             out[s, b, ST:, :] = out[s, b, ST:, :] + flags * pick[which, ST:, :]
 
-    def finish_q(n, carry):
-        b = 4 + n
-        i, j = b // 2, lax.rem(b, 2)
-        h = n // 2
+    def await_q(n, b):
+        h, j = n // 2, lax.rem(n, 2)
 
         @pl.when(j == o)
         def _():
-            arrival(cross.at[0, b, 1], e_r.at[i]).wait_recv()
+            arrival(cross.at[0, b, 1], e_r.at[b // 2]).wait_recv()
 
         @pl.when((j == o) & has_right)
         def _():
-            part = pl.ds(3 - k, 2)
-            arrival(cross.at[0, b, part], d_r.at[h]).wait_recv()
+            arrival(cross.at[0, b, pl.ds(3 - k, 2)], d_r.at[h]).wait_recv()
 
         @pl.when(swaps & has_right)
         def _():
             arrival(got_q.at[n], q_r.at[n]).wait_recv()
 
+    def finish_q(n):
+        b = turn(n // 2, lax.rem(n, 2))
+        await_q(n, b)
         pick[1] = cross[0, b, 0]
         pick[2] = cross[0, b, 1]
         pick[4] = cross[0, b, 3]
         pick[pl.ds(3 + 2 * o, 1)] = cross[0, b, pl.ds(2 + 2 * o, 1)]
         pick[pl.ds(3 + 2 * k, 1)] = got_q[pl.ds(n, 1)].astype(jnp.float32)
         combine(b)
-        return carry
-
-    lax.fori_loop(0, 4, finish_q, 0)
+
+    for c in range(2):
+
+        @pl.when(has_left & (k == 0))
+        def _():
+            half_products(c)
+
+        finish_q(c)
+
+        @pl.when(has_left & (k == 0))
+        def _():
+            for n in range(2):
+                return_m(c, n).start()
+
+    finish_q(3)
 
     def finish_p(b, carry):
         i, j = b // 2, lax.rem(b, 2)
@@ -371,6 +489,21 @@
 
     lax.fori_loop(0, 4, finish_p, 0)
 
+    await_q(2, CUT)
+
+    @pl.when(has_right)
+    def _():
+        for c in range(2):
+            arrival(got_m.at[:, :, pl.ds(c * HR, HR)], m_r.at[c]).wait_recv()
+
+    pick[1] = cross[0, CUT, 0]
+    pick[2] = cross[0, CUT, 1]
+    for n in range(3):
+        partial = got_m[n].reshape(2 * ST, ST).astype(jnp.float32)
+        near = got_q[2].astype(jnp.float32)
+        pick[3 + n] = partial + jnp.where(k * 2 == n, near, cross[0, CUT, 2 + n])
+    combine(CUT)
+
     for i in range(4):
         die(i).wait_send()
         hand_e(i, 2 * i + k).wait_send()
@@ -388,12 +521,20 @@
             for n in range(2):
                 return_p(h, n).wait_send()
 
+    @pl.when(has_left & (k == 0))
+    def _():
+        for c in range(2):
+            for n in range(2):
+                return_m(c, n).wait_send()
+
     @pl.when(has_right)
     def _():
         for b in range(4):
             across(b).wait_send()
         for h in range(2):
-            hand_d(h, 4 + 2 * h + k, o).wait_send()
+            hand_d(h, turn(h, k), o).wait_send()
+        for c in range(2):
+            half(c).wait_send()
 
     for h in range(2):
 
@@ -409,7 +550,7 @@
 def body(spectra, partner_codes, range_bits, old_stacks):
     codes = partner_codes.reshape(SLOTS)
     bits = jnp.transpose(range_bits, (0, 2, 4, 1, 3)).reshape(SLOTS * WORDS, 1, ST)
-    blocks = spectra.reshape(SEG, 2 * ST, BANDS * BW)
+    blocks = spectra.reshape(SEG, 2, ST, BANDS * BW)
     old = old_stacks.reshape(SLOTS, BANDS, 2 * ST, ST)
     dma = pltpu.SemaphoreType.DMA
     updated = pl.pallas_call(
@@ -423,7 +564,7 @@
         ],
         out_specs=pl.BlockSpec(memory_space=pltpu.VMEM),
         scratch_shapes=[
-            pltpu.VMEM((PLACES, SEG, 2 * ST, BW), jnp.bfloat16),
+            pltpu.VMEM((PLACES, SEG, 2, ST, BW), jnp.bfloat16),
             pltpu.VMEM((2, BANDS, SLOTS, 2 * ST, ST), jnp.float32),
             pltpu.VMEM((SLOTS, ST, ST), jnp.float32),
             pltpu.VMEM((SLOTS + 1, 2 * ST, ST), jnp.float32),
@@ -431,10 +572,14 @@
             pltpu.VMEM((4, 3, 2 * ST, ST), jnp.bfloat16),
             pltpu.VMEM((2, 2, 2 * ST, ST), jnp.bfloat16),
             pltpu.VMEM((4, 2 * ST, ST), jnp.bfloat16),
+            pltpu.VMEM((2, 3, 2, ST, ST), jnp.bfloat16),
+            pltpu.VMEM((3, 2, ST, ST), jnp.bfloat16),
             dma((BANDS,)), dma((BANDS,)),
             dma((4,)), dma((4,)), dma((8,)), dma((8,)), dma((8,)), dma((8,)),
             dma((2, 2)), dma((4,)), dma((2, 2)), dma((4,)),
             dma((4,)), dma((4,)), dma((2,)), dma((2,)),
+            dma((2,)), dma((2, 2)), dma((2, 2)), dma((2,)),
+            pltpu.SemaphoreType.REGULAR, pltpu.SemaphoreType.REGULAR,
         ],
         compiler_params=pltpu.CompilerParams(
             collective_id=0, has_side_effects=True, vmem_limit_bytes=52 * 1024 * 1024

time: 93.8 us -> 97.5 us (1.039)
  the two profiles are of different devices: /device:TPU:1 before, /device:TPU:97 now
where the time goes in v4:
time: 97.5 us; the launch traced here: 97.4 us
  Pallas kernels  95 us (97%)
  local copies, waits for them, and re-layouts  2.36 us (2%)
    pallas_call x1, Pallas kernels, body(): pl.pallas_call(kernel, out_shape=pltpu.VMEM((SLOTS, BANDS, 2 * ST, ST), j...  95 us
    unnamed x1, local copies, waits for them, and re-layouts  2.36 us

profile of v4, /device:TPU:97, one launch (start us, length us, event | category | flops | bytes accessed | tf_op | source)
XLA Modules:
  0.0 97.4 jit_solution(363260316798660645)
XLA Ops:
  0.0 95.0 %shard_map.46 = f32[5,8,256,128]{3,2,1,0:T(8,128)S(1)} custom-call(s32[5]{0:T(128)} %bitcast.11, s32[25,1,128]{2,1,0:T(1,128)} %bitcast.10, bf16[3,2,128,4096]{3,2,1,0:T(8,128)(2,1)} %bitcast.8, f32[5,8,256,128]{3,2,1,0:T(8,128)} %bitcast.9), custom_call_target="tpu_custom_call" | custom-call | tf_op jit(solution)/shard_map/pallas_call | solution.py:556
  95.0 2.4 %copy.6 = f32[1,1,5,8,2,128,128]{6,5,4,3,2,1,0:T(8,128)} copy(f32[1,1,5,8,2,128,128]{6,5,4,3,2,1,0:T(8,128)S(1)} %bitcast.7) | data formatting | bytes 10485760

commit v5 on v4

--- a/solution.py
+++ b/solution.py
@@ -82,10 +82,6 @@
     has_left, has_right = gy > 0, gy < COLS - 1
     has_above, has_below = base > 0, base < ROWS - 2
     swaps = jnp.where(k == 0, base > 0, base < ROWS - 2)
-    hears = jnp.where(k == 0, base < ROWS - 2, base > 0)
-
-    def band(b):
-        return spectra.at[:, :, :, pl.ds(pl.multiple_of(b * BW, BW), BW)]
 
     def remote(src, dst, send, recv, row, col):
         return pltpu.make_async_remote_copy(
@@ -94,13 +90,16 @@
         )
 
     def load(b):
-        return pltpu.make_async_copy(band(b), w.at[OWN + b], load_sem.at[b])
+        bins = pl.ds(b * BW, BW)
+        return pltpu.make_async_copy(spectra.at[:, :, :, bins], w.at[OWN + b], load_sem.at[b])
 
     def load_old(b):
         return pltpu.make_async_copy(old.at[:, b], out.at[:, b], old_sem.at[b])
 
     def die(i):
-        return remote(band(2 * i + o), w.at[OTHER + i], die_s.at[i], die_r.at[i], base + o, gy)
+        return remote(
+            w.at[OWN + 2 * i + o], w.at[OTHER + i], die_s.at[i], die_r.at[i], base + o, gy
+        )
 
     def across(b):
         if b == CUT:
@@ -113,7 +112,7 @@
         h, j = {0: 0, 1: 0, 2: 1, 3: 1, 6: 0, 5: 0, 7: 1}[b], b % 2
         at = (LEFT if b < CUT else RIGHT) + 2 * h + k
         return remote(
-            band(b), w.at[at], row_s.at[b], row_r.at[at - LEFT],
+            w.at[OWN + b], w.at[at], row_s.at[b], row_r.at[at - LEFT],
             base + j, right if b < CUT else left,
         )
 
@@ -131,11 +130,15 @@
             base + i, left,
         )
 
-    def vertical(b):
-        i, j = b // 2, b % 2
-        at = LOWER - 4 * k + i
-        chip = jnp.where(k == 0, above, below)
-        return remote(band(b), w.at[at], col_s.at[b], col_r.at[at - UPPER], chip + j, gy)
+    def chip_block(a, i):
+        return jnp.where(a == k, OWN + 2 * i + k, OTHER + i)
+
+    def vertical(a, i):
+        row, at = (above, LOWER) if a == 0 else (below, UPPER)
+        return remote(
+            w.at[chip_block(a, i)], w.at[at + i], col_s.at[a, i], col_r.at[at + i - UPPER],
+            row + k, gy,
+        )
 
     def return_p(h, i):
         return remote(
@@ -179,52 +182,90 @@
     greet(has_below, barrier, below, gy)
     greet(has_below & (k == 1), barrier, below + 1, gy)
 
-    def start_load(b, carry):
-        load(lax.rem(b + CUT, BANDS)).start()
-        return carry
-
-    lax.fori_loop(0, BANDS, start_load, 0)
-    pl.semaphore_wait(barrier, 1 + 2 * count(has_left) + (2 - k) * count(has_above))
-    for n in range(2):
-        greet(has_left, ready_right, base + n, left)
-    greet(has_above, ready_below, above + 1, gy)
-    greet(has_above & (k == 0), ready_below, above, gy)
-
-    vertical_order = (0, 5, 1, 7, 2, 6, 4, 3)
-
-    @pl.when(has_left)
-    def _():
-        for b in (5, 7, 6):
-            across(b).start()
-
-    @pl.when(has_above & (k == 0))
-    def _():
-        for b in vertical_order:
-            vertical(b).start()
-
-    for i in (0, 3, 2, 1):
-        die(i).start()
-
-    @pl.when(has_right)
-    def _():
-        pl.semaphore_wait(ready_right, 2)
-        for b in range(4):
-            across(b).start()
-
-    @pl.when(has_below)
-    def _():
-        pl.semaphore_wait(ready_below, 1 + k)
-
-    @pl.when(has_below & (k == 1))
-    def _():
-        for b in vertical_order:
-            vertical(b).start()
+    order = (5, 0, 1, 6, 7, 2, CUT, 3)
+    for b in order:
+        load(b).start()
+
+    def answer():
+        pl.semaphore_wait(barrier, 1 + 2 * count(has_left) + (2 - k) * count(has_above))
+        for n in range(2):
+            greet(has_left, ready_right, base + n, left)
+        greet(has_above, ready_below, above + 1, gy)
+        greet(has_above & (k == 0), ready_below, above, gy)
+
+    def send(b):
+        if b > CUT:
+
+            @pl.when(has_left)
+            def _():
+                across(b).start()
+
+        @pl.when(k != b % 2)
+        def _():
+            die(b // 2).start()
+
+        there = has_above if b % 2 == 0 else has_below
+
+        @pl.when(there & (k == b % 2))
+        def _():
+            vertical(b % 2, b // 2).start()
+
+        if b < CUT:
+
+            @pl.when(has_right)
+            def _():
+                across(b).start()
+
+        if b == CUT:
+
+            @pl.when(has_left)
+            def _():
+                across(b).start()
+
+    for n, b in enumerate(order):
+        load(b).wait()
+        whiten(w, OWN + b)
+        if n == 1:
+            answer()
+
+            @pl.when(has_right)
+            def _():
+                pl.semaphore_wait(ready_right, 2)
+
+            @pl.when(has_below)
+            def _():
+                pl.semaphore_wait(ready_below, 1 + k)
+
+        if n >= 1:
+            send(order[n - 1])
 
     def start_old(b, carry):
         load_old(b).start()
         return carry
 
     lax.fori_loop(0, BANDS, start_old, 0)
+
+    send(order[-1])
+
+    @pl.when(has_right)
+    def _():
+        for c in range(2):
+            half(c).start()
+
+    def pass_on(a):
+        for n in range(4):
+            i = ((2, 0, 3, 1), (0, 3, 1, 2))[a][n]
+            arrival(w.at[OTHER + i], die_r.at[i]).wait_recv()
+
+            @pl.when(has_below if a == 1 else has_above)
+            def _():
+                vertical(a, i).start()
+
+    for a in range(2):
+
+        @pl.when(a != k)
+        def _():
+            pass_on(a)
 
     column = lax.broadcasted_iota(jnp.int32, (ST, ST), 0)
     word = column // 30
@@ -237,22 +278,7 @@
         mask[s] = flags.T
     pick[0] = jnp.zeros((2 * ST, ST), jnp.float32)
 
-    def own_band(n, carry):
-        b = lax.rem(n + CUT, BANDS)
-        load(b).wait()
-        whiten(w, OWN + b)
-
-        @pl.when(n == 1)
-        def _():
-            @pl.when(has_left)
-            def _():
-                across(CUT).start()
-
-            @pl.when(has_right)
-            def _():
-                for c in range(2):
-                    half(c).start()
-
+    def own_band(b, carry):
         real, imag = pair(w, OWN + b, OWN + b)
         cross[0, b, 0, :ST, :] = real
         cross[0, b, 0, ST:, :] = imag
@@ -265,17 +291,12 @@
         for n in range(2):
             w[RIGHT + 2 + n, :, :, :, :HB] = jnp.zeros((SEG, 2, ST, HB), jnp.bfloat16)
 
-    def chip_block(a, i):
-        return jnp.where(a == k, OWN + 2 * i + k, OTHER + i)
-
     def put(owner, b, code, value):
         side = jnp.where(owner == k, 0, 1)
         cross[side, b, code, :ST, :] = value[0]
         cross[side, b, code, ST:, :] = value[1]
 
     def common(i):
-        arrival(w.at[OTHER + i], die_r.at[i]).wait_recv()
-
         @pl.when(has_above)
         def _():
             arrival(w.at[UPPER + i], col_r.at[i]).wait_recv()
@@ -283,19 +304,6 @@
         @pl.when(has_below)
         def _():
             arrival(w.at[LOWER + i], col_r.at[4 + i]).wait_recv()
-
-        def whiten_one(n, carry):
-            whiten(w, OTHER + 4 * n + i)
-            return carry
-
-        lax.fori_loop(0, 3, whiten_one, 0)
-
-    def whiten_two(place):
-        def whiten_one(n, carry):
-            whiten(w, place + n)
-            return carry
-
-        lax.fori_loop(0, 2, whiten_one, 0)
 
     def own_column(i):
         def below_pair(a, carry):
@@ -309,7 +317,6 @@
     def from_left(h, i):
         for n in range(2):
             arrival(w.at[LEFT + 2 * h + n], row_r.at[2 * h + n]).wait_recv()
-        whiten_two(LEFT + 2 * h)
 
         def left_pair(n, carry):
             own, a = n // 2, n % 2
@@ -341,7 +348,6 @@
         def _():
             for n in range(2):
                 arrival(w.at[RIGHT + 2 * h + n], row_r.at[4 + 2 * h + n]).wait_recv()
-            whiten_two(RIGHT + 2 * h)
 
         def right_corner(n, carry):
             real, imag = pair(w, UPPER + 4 * n + i, RIGHT + 2 * h + n)
@@ -358,16 +364,6 @@
 
         lax.fori_loop(0, 4, right_pair, 0)
 
-        @pl.when(has_above)
-        def _():
-            return_q(h, 0).start()
-
-        @pl.when(has_below)
-        def _():
-            return_q(h, 1).start()
-
-        hand_d(h, b, o).start()
-
     def stage(h, carry):
         common(h)
 
@@ -384,15 +380,31 @@
 
         b = turn(h, k)
         i = b // 2
+        common(i)
+
+        @pl.when(has_right)
+        def _():
+            from_right(h, i, b)
+
         hand_e(h, 2 * h + k).start()
-        common(i)
         own_column(i)
 
         @pl.when(has_right)
         def _():
-            from_right(h, i, b)
-
-        hand_e(i, b).start()
+            hand_d(h, b, o).start()
+
+        @pl.when(has_right & has_above)
+        def _():
+            return_q(h, 0).start()
+
+        @pl.when(has_right & has_below)
+        def _():
+            return_q(h, 1).start()
+
+        @pl.when(h == 1)
+        def _():
+            hand_e(turn(0, k) // 2, turn(0, k)).start()
+
         return carry
 
     lax.fori_loop(0, 2, stage, 0)
@@ -461,6 +473,8 @@
             half_products(c)
 
         finish_q(c)
+        if c == 0:
+            hand_e(turn(1, k) // 2, turn(1, k)).start()
 
         @pl.when(has_left & (k == 0))
         def _():
@@ -508,10 +522,15 @@
         die(i).wait_send()
         hand_e(i, 2 * i + k).wait_send()
 
-    @pl.when(swaps)
-    def _():
-        for b in range(BANDS):
-            vertical(b).wait_send()
+    @pl.when(has_above)
+    def _():
+        for i in range(4):
+            vertical(0, i).wait_send()
+
+    @pl.when(has_below)
+    def _():
+        for i in range(4):
+            vertical(1, i).wait_send()
 
     @pl.when(has_left)
     def _():
@@ -575,7 +594,7 @@
             pltpu.VMEM((2, 3, 2, ST, ST), jnp.bfloat16),
             pltpu.VMEM((3, 2, ST, ST), jnp.bfloat16),
             dma((BANDS,)), dma((BANDS,)),
-            dma((4,)), dma((4,)), dma((8,)), dma((8,)), dma((8,)), dma((8,)),
+            dma((4,)), dma((4,)), dma((8,)), dma((8,)), dma((2, 4)), dma((8,)),
             dma((2, 2)), dma((4,)), dma((2, 2)), dma((4,)),
             dma((4,)), dma((4,)), dma((2,)), dma((2,)),
             dma((2,)), dma((2, 2)), dma((2, 2)), dma((2,)),

time: 97.5 us -> 96.4 us (0.989)
  the two profiles are of different devices: /device:TPU:97 before, /device:TPU:1 now
where the time goes in v5:
time: 96.4 us; the launch traced here: 95.7 us
  Pallas kernels  93.4 us (97%)
  local copies, waits for them, and re-layouts  2.36 us (2%)
    pallas_call x1, Pallas kernels, body(): pl.pallas_call(kernel, out_shape=pltpu.VMEM((SLOTS, BANDS, 2 * ST, ST), j...  93.4 us
    unnamed x1, local copies, waits for them, and re-layouts  2.36 us

profile of v5, /device:TPU:1, one launch (start us, length us, event | category | flops | bytes accessed | tf_op | source)
XLA Modules:
  0.0 95.7 jit_solution(10562873920455310616)
XLA Ops:
  0.0 93.4 %shard_map.46 = f32[5,8,256,128]{3,2,1,0:T(8,128)S(1)} custom-call(s32[5]{0:T(128)} %bitcast.11, s32[25,1,128]{2,1,0:T(1,128)} %bitcast.10, bf16[3,2,128,4096]{3,2,1,0:T(8,128)(2,1)} %bitcast.8, f32[5,8,256,128]{3,2,1,0:T(8,128)} %bitcast.9), custom_call_target="tpu_custom_call" | custom-call | tf_op jit(solution)/shard_map/pallas_call | solution.py:575
  93.4 2.4 %copy.6 = f32[1,1,5,8,2,128,128]{6,5,4,3,2,1,0:T(8,128)} copy(f32[1,1,5,8,2,128,128]{6,5,4,3,2,1,0:T(8,128)S(1)} %bitcast.7) | data formatting | bytes 10485760

commit v6 on v5

--- a/solution.py
+++ b/solution.py
@@ -21,11 +21,12 @@
 
 OWN, OTHER, UPPER, LOWER, LEFT, RIGHT, HALF, PLACES = 0, 8, 12, 16, 20, 24, 28, 30
 CUT = 4
+RAW = (0, 5)
 HB = BW // 2
 HR = ST // 2
 
 
-def whiten(w, place):
+def whiten(w, place, first=0, last=ST // 16):
     def rows_of(t, carry):
         rows = pl.ds(pl.multiple_of(t * 16, 16), 16)
         total = jnp.zeros((16, BW), jnp.float32)
@@ -41,7 +42,7 @@
                 w[place, s, c, rows, :] = (x * gain).astype(jnp.bfloat16)
         return carry
 
-    lax.fori_loop(0, ST // 16, rows_of, 0, unroll=4)
+    lax.fori_loop(first, last, rows_of, 0, unroll=4)
 
 
 def pair(w, x, y, first=0, rows=ST, bins=BW):
@@ -112,7 +113,8 @@
         h, j = {0: 0, 1: 0, 2: 1, 3: 1, 6: 0, 5: 0, 7: 1}[b], b % 2
         at = (LEFT if b < CUT else RIGHT) + 2 * h + k
         return remote(
-            w.at[OWN + b], w.at[at], row_s.at[b], row_r.at[at - LEFT],
+            spectra.at[:, :, :, pl.ds(b * BW, BW)] if b in RAW else w.at[OWN + b],
+            w.at[at], row_s.at[b], row_r.at[at - LEFT],
             base + j, right if b < CUT else left,
         )
 
@@ -182,62 +184,59 @@
     greet(has_below, barrier, below, gy)
     greet(has_below & (k == 1), barrier, below + 1, gy)
 
-    order = (5, 0, 1, 6, 7, 2, CUT, 3)
+    order = (0, 5, 1, 6, 2, 3, CUT, 7)
     for b in order:
         load(b).start()
 
-    def answer():
-        pl.semaphore_wait(barrier, 1 + 2 * count(has_left) + (2 - k) * count(has_above))
-        for n in range(2):
-            greet(has_left, ready_right, base + n, left)
-        greet(has_above, ready_below, above + 1, gy)
-        greet(has_above & (k == 0), ready_below, above, gy)
+    pl.semaphore_wait(barrier, 1 + 2 * count(has_left) + (2 - k) * count(has_above))
+    for n in range(2):
+        greet(has_left, ready_right, base + n, left)
+    greet(has_above, ready_below, above + 1, gy)
+    greet(has_above & (k == 0), ready_below, above, gy)
+
+    @pl.when(has_left)
+    def _():
+        across(5).start()
+
+    @pl.when(has_right)
+    def _():
+        pl.semaphore_wait(ready_right, 2)
+        across(0).start()
+
+    @pl.when(has_below)
+    def _():
+        pl.semaphore_wait(ready_below, 1 + k)
 
     def send(b):
-        if b > CUT:
-
-            @pl.when(has_left)
+        @pl.when(k != b % 2)
+        def _():
+            die(b // 2).start()
+
+        there = has_above if b % 2 == 0 else has_below
+
+        @pl.when(there & (k == b % 2))
+        def _():
+            vertical(b % 2, b // 2).start()
+
+        if b not in RAW:
+
+            @pl.when(has_right if b < CUT else has_left)
             def _():
                 across(b).start()
 
-        @pl.when(k != b % 2)
-        def _():
-            die(b // 2).start()
-
-        there = has_above if b % 2 == 0 else has_below
-
-        @pl.when(there & (k == b % 2))
-        def _():
-            vertical(b % 2, b // 2).start()
-
-        if b < CUT:
+        if b == CUT:
 
             @pl.when(has_right)
             def _():
-                across(b).start()
-
-        if b == CUT:
-
-            @pl.when(has_left)
-            def _():
-                across(b).start()
+                for c in range(2):
+                    half(c).start()
 
     for n, b in enumerate(order):
         load(b).wait()
-        whiten(w, OWN + b)
-        if n == 1:
-            answer()
-
-            @pl.when(has_right)
-            def _():
-                pl.semaphore_wait(ready_right, 2)
-
-            @pl.when(has_below)
-            def _():
-                pl.semaphore_wait(ready_below, 1 + k)
-
+        whiten(w, OWN + b, 0, 4)
         if n >= 1:
             send(order[n - 1])
+        whiten(w, OWN + b, 4, 8)
 
     def start_old(b, carry):
         load_old(b).start()
@@ -247,14 +246,9 @@
 
     send(order[-1])
 
-    @pl.when(has_right)
-    def _():
-        for c in range(2):
-            half(c).start()
-
     def pass_on(a):
         for n in range(4):
-            i = ((2, 0, 3, 1), (0, 3, 1, 2))[a][n]
+            i = ((2, 0, 1, 3), (0, 3, 1, 2))[a][n]
             arrival(w.at[OTHER + i], die_r.at[i]).wait_recv()
 
             @pl.when(has_below if a == 1 else has_above)
@@ -314,26 +308,37 @@
 
         lax.fori_loop(0, 2, below_pair, 0)
 
+    def whiten_two(place):
+        def whiten_one(n, carry):
+            whiten(w, place + n)
+            return carry
+
+        lax.fori_loop(0, 2, whiten_one, 0)
+
+    def partner(own, t, i):
+        corner = t == 2
+        y = jnp.where(corner, UPPER + 4 * own + i, chip_block(t, i))
+        return y, jnp.where(corner, 2 * own, 1 + t - own)
+
     def from_left(h, i):
         for n in range(2):
             arrival(w.at[LEFT + 2 * h + n], row_r.at[2 * h + n]).wait_recv()
 
+        @pl.when((h == 0) & (k == 0))
+        def _():
+            whiten_two(LEFT)
+
         def left_pair(n, carry):
-            own, a = n // 2, n % 2
-            real, imag = pair(w, LEFT + 2 * h + own, chip_block(a, i))
-            sent_p[h, own, 1 + a - own, :ST, :] = real.astype(jnp.bfloat16)
-            sent_p[h, own, 1 + a - own, ST:, :] = imag.astype(jnp.bfloat16)
+            own, t = n // 3, n % 3
+            y, code = partner(own, t, i)
+            real, imag = pair(w, LEFT + 2 * h + own, y)
+            sent_p[h, own, code, :ST, :] = real.astype(jnp.bfloat16)
+            sent_p[h, own, code, ST:, :] = imag.astype(jnp.bfloat16)
             return carry
 
-        lax.fori_loop(0, 4, left_pair, 0)
-
-        def left_corner(own, carry):
-            real, imag = pair(w, LEFT + 2 * h + own, UPPER + 4 * own + i)
-            sent_p[h, own, 2 * own, :ST, :] = real.astype(jnp.bfloat16)
-            sent_p[h, own, 2 * own, ST:, :] = imag.astype(jnp.bfloat16)
-            return carry
-
-        lax.fori_loop(0, 2, left_corner, 0)
+        lax.fori_loop(0, 6, left_pair, 0)
+        for n in range(2):
+            return_p(h, n).start()
 
     def from_right(h, i, b):
         cut = (h == 1) & (k == 0)
@@ -348,6 +353,10 @@
         def _():
             for n in range(2):
                 arrival(w.at[RIGHT + 2 * h + n], row_r.at[4 + 2 * h + n]).wait_recv()
+
+        @pl.when((h == 0) & (k == 1))
+        def _():
+            whiten_two(RIGHT)
 
         def right_corner(n, carry):
             real, imag = pair(w, UPPER + 4 * n + i, RIGHT + 2 * h + n)
@@ -372,12 +381,6 @@
             from_left(h, h)
 
         own_column(h)
-
-        @pl.when(has_left)
-        def _():
-            for n in range(2):
-                return_p(h, n).start()
-
         b = turn(h, k)
         i = b // 2
         common(i)
@@ -415,23 +418,17 @@
             part = w.at[HALF + n, :, :, pl.ds(c * HR, HR), pl.ds(0, HB)]
             arrival(part, half_r.at[c, n]).wait_recv()
 
-        def half_put(own, code, y):
+        def half_pair(n, carry):
+            own, t = n // 3, n % 3
+            y, code = partner(own, t, i)
             real, imag = pair(w, HALF + own, y, c * HR, HR, HB)
             sent_m[own, code, 0, c * HR:(c + 1) * HR, :] = real.astype(jnp.bfloat16)
             sent_m[own, code, 1, c * HR:(c + 1) * HR, :] = imag.astype(jnp.bfloat16)
-
-        def half_pair(n, carry):
-            own, a = n // 2, n % 2
-            half_put(own, 1 + a - own, chip_block(a, i))
             return carry
 
-        lax.fori_loop(0, 4, half_pair, 0)
-
-        def half_corner(own, carry):
-            half_put(own, 2 * own, UPPER + 4 * own + i)
-            return carry
-
-        lax.fori_loop(0, 2, half_corner, 0)
+        lax.fori_loop(0, 6, half_pair, 0)
+        for n in range(2):
+            return_m(c, n).start()
 
     def combine(b):
         load_old(b).wait()
@@ -466,20 +463,14 @@
         pick[pl.ds(3 + 2 * k, 1)] = got_q[pl.ds(n, 1)].astype(jnp.float32)
         combine(b)
 
-    for c in range(2):
-
-        @pl.when(has_left & (k == 0))
-        def _():
+    finish_q(0)
+    hand_e(turn(1, k) // 2, turn(1, k)).start()
+    finish_q(1)
+
+    @pl.when(has_left & (k == 0))
+    def _():
+        for c in range(2):
             half_products(c)
-
-        finish_q(c)
-        if c == 0:
-            hand_e(turn(1, k) // 2, turn(1, k)).start()
-
-        @pl.when(has_left & (k == 0))
-        def _():
-            for n in range(2):
-                return_m(c, n).start()
 
     finish_q(3)
 

time: 96.4 us -> 97.3 us (level)
  the two profiles are of different devices: /device:TPU:1 before, /device:TPU:47 now
where the time goes in v6:
time: 97.3 us; the launch traced here: 97.2 us
  Pallas kernels  94.8 us (97%)
  local copies, waits for them, and re-layouts  2.36 us (2%)
    pallas_call x1, Pallas kernels, body(): pl.pallas_call(kernel, out_shape=pltpu.VMEM((SLOTS, BANDS, 2 * ST, ST), j...  94.8 us
    unnamed x1, local copies, waits for them, and re-layouts  2.36 us

profile of v6, /device:TPU:47, one launch (start us, length us, event | category | flops | bytes accessed | tf_op | source)
XLA Modules:
  0.0 97.2 jit_solution(4312287508450952589)
XLA Ops:
  0.0 94.8 %shard_map.46 = f32[5,8,256,128]{3,2,1,0:T(8,128)S(1)} custom-call(s32[5]{0:T(128)} %bitcast.11, s32[25,1,128]{2,1,0:T(1,128)} %bitcast.10, bf16[3,2,128,4096]{3,2,1,0:T(8,128)(2,1)} %bitcast.8, f32[5,8,256,128]{3,2,1,0:T(8,128)} %bitcast.9), custom_call_target="tpu_custom_call" | custom-call | tf_op jit(solution)/shard_map/pallas_call | solution.py:566
  94.8 2.4 %copy.6 = f32[1,1,5,8,2,128,128]{6,5,4,3,2,1,0:T(8,128)} copy(f32[1,1,5,8,2,128,128]{6,5,4,3,2,1,0:T(8,128)S(1)} %bitcast.7) | data formatting | bytes 10485760

commit v7 on v6

--- a/solution.py
+++ b/solution.py
@@ -22,7 +22,6 @@
 OWN, OTHER, UPPER, LOWER, LEFT, RIGHT, HALF, PLACES = 0, 8, 12, 16, 20, 24, 28, 30
 CUT = 4
 RAW = (0, 5)
-HB = BW // 2
 HR = ST // 2
 
 
@@ -45,12 +44,12 @@
     lax.fori_loop(first, last, rows_of, 0, unroll=4)
 
 
-def pair(w, x, y, first=0, rows=ST, bins=BW):
+def pair(w, x, y, first=0, rows=ST, segments=SEG):
     total = None
-    for s in range(SEG):
+    for s in range(segments):
         part = lax.dot_general(
-            w[x, s, :, first:first + rows, :bins].reshape(2 * rows, bins),
-            w[y, s, :, :, :bins].reshape(2 * ST, bins),
+            w[x, s, :, first:first + rows].reshape(2 * rows, BW),
+            w[y, s].reshape(2 * ST, BW),
             (((1,), (1,)), ((), ())), preferred_element_type=jnp.float32,
         )
         total = part if total is None else total + part
@@ -67,9 +66,9 @@
     codes, bits, spectra, old, out,
     w, cross, mask, pick, sent_p, got_p, sent_q, got_q, sent_m, got_m,
     load_sem, old_sem,
-    die_s, die_r, row_s, row_r, col_s, col_r,
+    die_s, die_r, left_s, left_r, right_s, right_r, col_s, col_r,
     p_s, p_r, q_s, q_r, e_s, e_r, d_s, d_r,
-    half_s, half_r, m_s, m_r, ready_right, ready_below,
+    m_s, m_r, ready_right, ready_below,
 ):
     gx = lax.axis_index("gx")
     gy = lax.axis_index("gy")
@@ -102,28 +101,29 @@
             w.at[OWN + 2 * i + o], w.at[OTHER + i], die_s.at[i], die_r.at[i], base + o, gy
         )
 
-    def across(b):
+    def leftward(b):
+        h, j = {6: 0, 5: 0, CUT: 1, 7: 1}[b], b % 2
+        at = RIGHT + 2 * h + k
         if b == CUT:
-            part = pl.ds(HB, HB)
-            at = RIGHT + 2 + k
-            return remote(
-                w.at[OWN + CUT, :, :, :, part], w.at[at, :, :, :, part],
-                row_s.at[b], row_r.at[at - LEFT], base, left,
-            )
-        h, j = {0: 0, 1: 0, 2: 1, 3: 1, 6: 0, 5: 0, 7: 1}[b], b % 2
-        at = (LEFT if b < CUT else RIGHT) + 2 * h + k
-        return remote(
-            spectra.at[:, :, :, pl.ds(b * BW, BW)] if b in RAW else w.at[OWN + b],
-            w.at[at], row_s.at[b], row_r.at[at - LEFT],
-            base + j, right if b < CUT else left,
-        )
-
-    def half(c):
-        rows, part = pl.ds(c * HR, HR), pl.ds(0, HB)
-        return remote(
-            w.at[OWN + CUT, :, :, rows, part], w.at[HALF + k, :, :, rows, part],
-            half_s.at[c], half_r.at[c, k], base, right,
-        )
+            src, dst = w.at[OWN + b, pl.ds(1, 2)], w.at[at, pl.ds(1, 2)]
+        else:
+            src = spectra.at[:, :, :, pl.ds(b * BW, BW)] if b in RAW else w.at[OWN + b]
+            dst = w.at[at]
+        return remote(src, dst, left_s.at[h, j], left_r.at[h, k], base + j, left)
+
+    def rightward(b, c):
+        rows = pl.ds(c * HR, HR)
+        h, j = b // 2, b % 2
+        if b == CUT:
+            src = w.at[OWN + b, pl.ds(0, 1), :, rows]
+            dst = w.at[HALF + k, pl.ds(0, 1), :, rows]
+        else:
+            dst = w.at[LEFT + 2 * h + k, :, :, rows]
+            if b in RAW:
+                src = spectra.at[:, :, rows, pl.ds(b * BW, BW)]
+            else:
+                src = w.at[OWN + b, :, :, rows]
+        return remote(src, dst, right_s.at[b, c], right_r.at[h, c, k], base + j, right)
 
     def return_m(c, i):
         rows = pl.ds(c * HR, HR)
@@ -142,10 +142,11 @@
             row + k, gy,
         )
 
-    def return_p(h, i):
+    def return_p(h, c, i):
+        rows = pl.ds(c * HR, HR)
         return remote(
-            sent_p.at[h, i], got_p.at[2 * h + k], p_s.at[h, i], p_r.at[2 * h + k],
-            base + i, left,
+            sent_p.at[h, i, :, :, rows], got_p.at[2 * h + k, :, :, rows],
+            p_s.at[h, c, i], p_r.at[2 * h + k, c], base + i, left,
         )
 
     def return_q(h, i):
@@ -196,12 +197,13 @@
 
     @pl.when(has_left)
     def _():
-        across(5).start()
+        leftward(5).start()
 
     @pl.when(has_right)
     def _():
         pl.semaphore_wait(ready_right, 2)
-        across(0).start()
+        for c in range(2):
+            rightward(0, c).start()
 
     @pl.when(has_below)
     def _():
@@ -218,18 +220,18 @@
         def _():
             vertical(b % 2, b // 2).start()
 
-        if b not in RAW:
-
-            @pl.when(has_right if b < CUT else has_left)
+        if b >= CUT and b not in RAW:
+
+            @pl.when(has_left)
             def _():
-                across(b).start()
-
-        if b == CUT:
+                leftward(b).start()
+
+        if b <= CUT and b not in RAW:
 
             @pl.when(has_right)
             def _():
                 for c in range(2):
-                    half(c).start()
+                    rightward(b, c).start()
 
     for n, b in enumerate(order):
         load(b).wait()
@@ -283,7 +285,7 @@
     @pl.when(k == 0)
     def _():
         for n in range(2):
-            w[RIGHT + 2 + n, :, :, :, :HB] = jnp.zeros((SEG, 2, ST, HB), jnp.bfloat16)
+            w[RIGHT + 2 + n, 0] = jnp.zeros((2, ST, BW), jnp.bfloat16)
 
     def put(owner, b, code, value):
         side = jnp.where(owner == k, 0, 1)
@@ -300,7 +302,8 @@
             arrival(w.at[LOWER + i], col_r.at[4 + i]).wait_recv()
 
     def own_column(i):
-        def below_pair(a, carry):
+        def below_pair(n, carry):
+            a = jnp.where(n == 0, o, k)
             x = chip_block(a, i)
             y = jnp.where(a == 0, chip_block(1, i), LOWER + i)
             put(a, 2 * i + k, 1, pair(w, x, y))
@@ -308,9 +311,9 @@
 
         lax.fori_loop(0, 2, below_pair, 0)
 
-    def whiten_two(place):
+    def whiten_two(place, first, last):
         def whiten_one(n, carry):
-            whiten(w, place + n)
+            whiten(w, place + n, first, last)
             return carry
 
         lax.fori_loop(0, 2, whiten_one, 0)
@@ -321,24 +324,26 @@
         return y, jnp.where(corner, 2 * own, 1 + t - own)
 
     def from_left(h, i):
-        for n in range(2):
-            arrival(w.at[LEFT + 2 * h + n], row_r.at[2 * h + n]).wait_recv()
-
-        @pl.when((h == 0) & (k == 0))
-        def _():
-            whiten_two(LEFT)
-
-        def left_pair(n, carry):
-            own, t = n // 3, n % 3
-            y, code = partner(own, t, i)
-            real, imag = pair(w, LEFT + 2 * h + own, y)
-            sent_p[h, own, code, :ST, :] = real.astype(jnp.bfloat16)
-            sent_p[h, own, code, ST:, :] = imag.astype(jnp.bfloat16)
-            return carry
-
-        lax.fori_loop(0, 6, left_pair, 0)
-        for n in range(2):
-            return_p(h, n).start()
+        for c in range(2):
+            for n in range(2):
+                part = w.at[LEFT + 2 * h + n, :, :, pl.ds(c * HR, HR)]
+                arrival(part, right_r.at[h, c, n]).wait_recv()
+
+            @pl.when((h == 0) & (k == 0))
+            def _():
+                whiten_two(LEFT, 4 * c, 4 * c + 4)
+
+            def left_pair(n, carry):
+                own, t = n // 3, n % 3
+                y, code = partner(own, t, i)
+                real, imag = pair(w, LEFT + 2 * h + own, y, c * HR, HR)
+                sent_p[h, own, code, 0, c * HR:(c + 1) * HR, :] = real.astype(jnp.bfloat16)
+                sent_p[h, own, code, 1, c * HR:(c + 1) * HR, :] = imag.astype(jnp.bfloat16)
+                return carry
+
+            lax.fori_loop(0, 6, left_pair, 0)
+            for n in range(2):
+                return_p(h, c, n).start()
 
     def from_right(h, i, b):
         cut = (h == 1) & (k == 0)
@@ -346,17 +351,16 @@
         @pl.when(cut)
         def _():
             for n in range(2):
-                part = w.at[RIGHT + 2 + n, :, :, :, pl.ds(HB, HB)]
-                arrival(part, row_r.at[6 + n]).wait_recv()
+                arrival(w.at[RIGHT + 2 + n, pl.ds(1, 2)], left_r.at[1, n]).wait_recv()
 
         @pl.when(jnp.logical_not(cut))
         def _():
             for n in range(2):
-                arrival(w.at[RIGHT + 2 * h + n], row_r.at[4 + 2 * h + n]).wait_recv()
+                arrival(w.at[RIGHT + 2 * h + n], left_r.at[h, n]).wait_recv()
 
         @pl.when((h == 0) & (k == 1))
         def _():
-            whiten_two(RIGHT)
+            whiten_two(RIGHT, 0, ST // 16)
 
         def right_corner(n, carry):
             real, imag = pair(w, UPPER + 4 * n + i, RIGHT + 2 * h + n)
@@ -367,7 +371,7 @@
         lax.fori_loop(0, 2, right_corner, 0)
 
         def right_pair(n, carry):
-            a, far = n // 2, n % 2
+            a, far = jnp.where(n < 2, o, k), n % 2
             put(a, b, 3 + far - a, pair(w, chip_block(a, i), RIGHT + 2 * h + far))
             return carry
 
@@ -381,6 +385,7 @@
             from_left(h, h)
 
         own_column(h)
+        hand_e(h, 2 * h + k).start()
         b = turn(h, k)
         i = b // 2
         common(i)
@@ -389,8 +394,8 @@
         def _():
             from_right(h, i, b)
 
-        hand_e(h, 2 * h + k).start()
         own_column(i)
+        hand_e(i, b).start()
 
         @pl.when(has_right)
         def _():
@@ -403,10 +408,6 @@
         @pl.when(has_right & has_below)
         def _():
             return_q(h, 1).start()
-
-        @pl.when(h == 1)
-        def _():
-            hand_e(turn(0, k) // 2, turn(0, k)).start()
 
         return carry
 
@@ -415,13 +416,13 @@
     def half_products(c):
         i = CUT // 2
         for n in range(2):
-            part = w.at[HALF + n, :, :, pl.ds(c * HR, HR), pl.ds(0, HB)]
-            arrival(part, half_r.at[c, n]).wait_recv()
+            part = w.at[HALF + n, pl.ds(0, 1), :, pl.ds(c * HR, HR)]
+            arrival(part, right_r.at[2, c, n]).wait_recv()
 
         def half_pair(n, carry):
             own, t = n // 3, n % 3
             y, code = partner(own, t, i)
-            real, imag = pair(w, HALF + own, y, c * HR, HR, HB)
+            real, imag = pair(w, HALF + own, y, c * HR, HR, 1)
             sent_m[own, code, 0, c * HR:(c + 1) * HR, :] = real.astype(jnp.bfloat16)
             sent_m[own, code, 1, c * HR:(c + 1) * HR, :] = imag.astype(jnp.bfloat16)
             return carry
@@ -463,15 +464,13 @@
         pick[pl.ds(3 + 2 * k, 1)] = got_q[pl.ds(n, 1)].astype(jnp.float32)
         combine(b)
 
-    finish_q(0)
-    hand_e(turn(1, k) // 2, turn(1, k)).start()
-    finish_q(1)
-
     @pl.when(has_left & (k == 0))
     def _():
         for c in range(2):
             half_products(c)
 
+    finish_q(0)
+    finish_q(1)
     finish_q(3)
 
     def finish_p(b, carry):
@@ -483,12 +482,13 @@
 
         @pl.when(has_right)
         def _():
-            arrival(got_p.at[b], p_r.at[b]).wait_recv()
+            for c in range(2):
+                arrival(got_p.at[b, :, :, pl.ds(c * HR, HR)], p_r.at[b, c]).wait_recv()
 
         pick[1] = cross[0, b, 0]
         pick[2] = cross[0, b, 1]
         for n in range(3):
-            pick[3 + n] = got_p[b, n].astype(jnp.float32)
+            pick[3 + n] = got_p[b, n].reshape(2 * ST, ST).astype(jnp.float32)
         combine(b)
         return carry
 
@@ -525,11 +525,12 @@
 
     @pl.when(has_left)
     def _():
-        for b in range(4):
-            across(4 + b).wait_send()
-        for h in range(2):
+        for b in range(CUT, BANDS):
+            leftward(b).wait_send()
+        for c in range(2):
             for n in range(2):
-                return_p(h, n).wait_send()
+                for h in range(2):
+                    return_p(h, c, n).wait_send()
 
     @pl.when(has_left & (k == 0))
     def _():
@@ -539,12 +540,11 @@
 
     @pl.when(has_right)
     def _():
-        for b in range(4):
-            across(b).wait_send()
+        for b in range(CUT + 1):
+            for c in range(2):
+                rightward(b, c).wait_send()
         for h in range(2):
             hand_d(h, turn(h, k), o).wait_send()
-        for c in range(2):
-            half(c).wait_send()
 
     for h in range(2):
 
@@ -578,17 +578,18 @@
             pltpu.VMEM((2, BANDS, SLOTS, 2 * ST, ST), jnp.float32),
             pltpu.VMEM((SLOTS, ST, ST), jnp.float32),
             pltpu.VMEM((SLOTS + 1, 2 * ST, ST), jnp.float32),
-            pltpu.VMEM((2, 2, 3, 2 * ST, ST), jnp.bfloat16),
-            pltpu.VMEM((4, 3, 2 * ST, ST), jnp.bfloat16),
+            pltpu.VMEM((2, 2, 3, 2, ST, ST), jnp.bfloat16),
+            pltpu.VMEM((4, 3, 2, ST, ST), jnp.bfloat16),
             pltpu.VMEM((2, 2, 2 * ST, ST), jnp.bfloat16),
             pltpu.VMEM((4, 2 * ST, ST), jnp.bfloat16),
             pltpu.VMEM((2, 3, 2, ST, ST), jnp.bfloat16),
             pltpu.VMEM((3, 2, ST, ST), jnp.bfloat16),
             dma((BANDS,)), dma((BANDS,)),
-            dma((4,)), dma((4,)), dma((8,)), dma((8,)), dma((2, 4)), dma((8,)),
-            dma((2, 2)), dma((4,)), dma((2, 2)), dma((4,)),
+            dma((4,)), dma((4,)), dma((2, 2)), dma((2, 2)), dma((5, 2)), dma((3, 2, 2)),
+            dma((2, 4)), dma((8,)),
+            dma((2, 2, 2)), dma((4, 2)), dma((2, 2)), dma((4,)),
             dma((4,)), dma((4,)), dma((2,)), dma((2,)),
-            dma((2,)), dma((2, 2)), dma((2, 2)), dma((2,)),
+            dma((2, 2)), dma((2,)),
             pltpu.SemaphoreType.REGULAR, pltpu.SemaphoreType.REGULAR,
         ],
         compiler_params=pltpu.CompilerParams(

time: 97.3 us -> 92.7 us (0.953)
  the two profiles are of different devices: /device:TPU:47 before, /device:TPU:1 now
where the time goes in v7:
time: 92.7 us; the launch traced here: 91.1 us
  Pallas kernels  88.7 us (96%)
  local copies, waits for them, and re-layouts  2.36 us (3%)
    pallas_call x1, Pallas kernels, body(): pl.pallas_call(kernel, out_shape=pltpu.VMEM((SLOTS, BANDS, 2 * ST, ST), j...  88.7 us
    unnamed x1, local copies, waits for them, and re-layouts  2.36 us

profile of v7, /device:TPU:1, one launch (start us, length us, event | category | flops | bytes accessed | tf_op | source)
XLA Modules:
  0.0 91.1 jit_solution(4916529056106145314)
XLA Ops:
  0.0 88.7 %shard_map.46 = f32[5,8,256,128]{3,2,1,0:T(8,128)S(1)} custom-call(s32[5]{0:T(128)} %bitcast.11, s32[25,1,128]{2,1,0:T(1,128)} %bitcast.10, bf16[3,2,128,4096]{3,2,1,0:T(8,128)(2,1)} %bitcast.8, f32[5,8,256,128]{3,2,1,0:T(8,128)} %bitcast.9), custom_call_target="tpu_custom_call" | custom-call | tf_op jit(solution)/shard_map/pallas_call | solution.py:566
  88.7 2.4 %copy.6 = f32[1,1,5,8,2,128,128]{6,5,4,3,2,1,0:T(8,128)} copy(f32[1,1,5,8,2,128,128]{6,5,4,3,2,1,0:T(8,128)S(1)} %bitcast.7) | data formatting | bytes 10485760

commit v8 on v7

--- a/solution.py
+++ b/solution.py
@@ -23,6 +23,10 @@
 CUT = 4
 RAW = (0, 5)
 HR = ST // 2
+HB = BW // 2
+PIECES = 4
+PR = ST // PIECES
+XLINE = 4
 
 
 def whiten(w, place, first=0, last=ST // 16):
@@ -44,18 +48,35 @@
     lax.fori_loop(first, last, rows_of, 0, unroll=4)
 
 
-def pair(w, x, y, first=0, rows=ST, segments=SEG):
+def pair(w, x, y, first=0, rows=ST, bins=BW):
     total = None
-    for s in range(segments):
+    for s in range(SEG):
         part = lax.dot_general(
-            w[x, s, :, first:first + rows].reshape(2 * rows, BW),
-            w[y, s].reshape(2 * ST, BW),
+            w[x, s, :, first:first + rows, :bins].reshape(2 * rows, bins),
+            w[y, s, :, :, :bins].reshape(2 * ST, bins),
             (((1,), (1,)), ((), ())), preferred_element_type=jnp.float32,
         )
         total = part if total is None else total + part
     real = (total[:rows, :ST] + total[rows:, ST:]) * SCALE
     imag = (total[rows:, :ST] - total[:rows, ST:]) * SCALE
     return real, imag
+
+
+def pairs(w, x, y, count, first, rows, bins):
+    total = None
+    for s in range(SEG):
+        part = lax.dot_general(
+            w[pl.ds(x, count), s, :, first:first + rows, :bins].reshape(count * 2 * rows, bins),
+            w[y, s, :, :, :bins].reshape(2 * ST, bins),
+            (((1,), (1,)), ((), ())), preferred_element_type=jnp.float32,
+        )
+        total = part if total is None else total + part
+    products = []
+    for n in range(count):
+        top = total[2 * n * rows:(2 * n + 1) * rows]
+        low = total[(2 * n + 1) * rows:(2 * n + 2) * rows]
+        products.append(((top[:, :ST] + low[:, ST:]) * SCALE, (low[:, :ST] - top[:, ST:]) * SCALE))
+    return products
 
 
 def turn(h, core):
@@ -68,7 +89,7 @@
     load_sem, old_sem,
     die_s, die_r, left_s, left_r, right_s, right_r, col_s, col_r,
     p_s, p_r, q_s, q_r, e_s, e_r, d_s, d_r,
-    m_s, m_r, ready_right, ready_below,
+    half_s, half_r, m_s, m_r, ready_right, ready_below,
 ):
     gx = lax.axis_index("gx")
     gy = lax.axis_index("gy")
@@ -80,6 +101,8 @@
     above = lax.rem(base + ROWS - 2, ROWS)
     below = lax.rem(base + 2, ROWS)
     has_left, has_right = gy > 0, gy < COLS - 1
+    wrap_left = has_left & (lax.rem(gy, XLINE) == 0)
+    wrap_right = has_right & (lax.rem(gy, XLINE) == XLINE - 1)
     has_above, has_below = base > 0, base < ROWS - 2
     swaps = jnp.where(k == 0, base > 0, base < ROWS - 2)
 
@@ -105,7 +128,8 @@
         h, j = {6: 0, 5: 0, CUT: 1, 7: 1}[b], b % 2
         at = RIGHT + 2 * h + k
         if b == CUT:
-            src, dst = w.at[OWN + b, pl.ds(1, 2)], w.at[at, pl.ds(1, 2)]
+            bins = pl.ds(HB, HB)
+            src, dst = w.at[OWN + b, :, :, :, bins], w.at[at, :, :, :, bins]
         else:
             src = spectra.at[:, :, :, pl.ds(b * BW, BW)] if b in RAW else w.at[OWN + b]
             dst = w.at[at]
@@ -114,19 +138,22 @@
     def rightward(b, c):
         rows = pl.ds(c * HR, HR)
         h, j = b // 2, b % 2
-        if b == CUT:
-            src = w.at[OWN + b, pl.ds(0, 1), :, rows]
-            dst = w.at[HALF + k, pl.ds(0, 1), :, rows]
+        dst = w.at[LEFT + 2 * h + k, :, :, rows]
+        if b in RAW:
+            src = spectra.at[:, :, rows, pl.ds(b * BW, BW)]
         else:
-            dst = w.at[LEFT + 2 * h + k, :, :, rows]
-            if b in RAW:
-                src = spectra.at[:, :, rows, pl.ds(b * BW, BW)]
-            else:
-                src = w.at[OWN + b, :, :, rows]
+            src = w.at[OWN + b, :, :, rows]
         return remote(src, dst, right_s.at[b, c], right_r.at[h, c, k], base + j, right)
 
+    def half(c):
+        rows, bins = pl.ds(c * PR, PR), pl.ds(0, HB)
+        return remote(
+            w.at[OWN + CUT, :, :, rows, bins], w.at[HALF + k, :, :, rows, bins],
+            half_s.at[c], half_r.at[c, k], base, right,
+        )
+
     def return_m(c, i):
-        rows = pl.ds(c * HR, HR)
+        rows = pl.ds(c * PR, PR)
         return remote(
             sent_m.at[i, :, :, rows], got_m.at[:, :, rows], m_s.at[c, i], m_r.at[c],
             base + i, left,
@@ -182,16 +209,18 @@
     pl.semaphore_signal(barrier, inc=1, device_id=(base + o, gy), device_id_type=MESH)
     for n in range(2):
         greet(has_right, barrier, base + n, right)
+        greet(wrap_left, barrier, base + n, left)
     greet(has_below, barrier, below, gy)
     greet(has_below & (k == 1), barrier, below + 1, gy)
 
     order = (0, 5, 1, 6, 2, 3, CUT, 7)
-    for b in order:
+    for b in order[:2]:
         load(b).start()
 
-    pl.semaphore_wait(barrier, 1 + 2 * count(has_left) + (2 - k) * count(has_above))
+    heard = 1 + 2 * (count(has_left) + count(wrap_right)) + (2 - k) * count(has_above)
+    pl.semaphore_wait(barrier, heard)
     for n in range(2):
-        greet(has_left, ready_right, base + n, left)
+        greet(has_left & jnp.logical_not(wrap_left), ready_right, base + n, left)
     greet(has_above, ready_below, above + 1, gy)
     greet(has_above & (k == 0), ready_below, above, gy)
 
@@ -199,11 +228,17 @@
     def _():
         leftward(5).start()
 
+    @pl.when(has_right & jnp.logical_not(wrap_right))
+    def _():
+        pl.semaphore_wait(ready_right, 2)
+
     @pl.when(has_right)
     def _():
-        pl.semaphore_wait(ready_right, 2)
         for c in range(2):
             rightward(0, c).start()
+
+    for b in order[2:]:
+        load(b).start()
 
     @pl.when(has_below)
     def _():
@@ -226,12 +261,19 @@
             def _():
                 leftward(b).start()
 
-        if b <= CUT and b not in RAW:
+        if b < CUT and b not in RAW:
 
             @pl.when(has_right)
             def _():
                 for c in range(2):
                     rightward(b, c).start()
+
+        if b == CUT:
+
+            @pl.when(has_right)
+            def _():
+                for c in range(PIECES):
+                    half(c).start()
 
     for n, b in enumerate(order):
         load(b).wait()
@@ -285,7 +327,7 @@
     @pl.when(k == 0)
     def _():
         for n in range(2):
-            w[RIGHT + 2 + n, 0] = jnp.zeros((2, ST, BW), jnp.bfloat16)
+            w[RIGHT + 2 + n, :, :, :, :HB] = jnp.zeros((SEG, 2, ST, HB), jnp.bfloat16)
 
     def put(owner, b, code, value):
         side = jnp.where(owner == k, 0, 1)
@@ -318,10 +360,18 @@
 
         lax.fori_loop(0, 2, whiten_one, 0)
 
-    def partner(own, t, i):
-        corner = t == 2
-        y = jnp.where(corner, UPPER + 4 * own + i, chip_block(t, i))
-        return y, jnp.where(corner, 2 * own, 1 + t - own)
+    def left_products(place, i, first, rows, bins, dst):
+        def store(own, code, value):
+            for n in range(2):
+                dst[own, code, n, first:first + rows, :] = value[n].astype(jnp.bfloat16)
+
+        for a in range(2):
+            both = pairs(w, place, chip_block(a, i), 2, first, rows, bins)
+            for own in range(2):
+                store(own, 1 + a - own, both[own])
+        for own in range(2):
+            corner = pairs(w, place + own, UPPER + 4 * own + i, 1, first, rows, bins)
+            store(own, 2 * own, corner[0])
 
     def from_left(h, i):
         for c in range(2):
@@ -333,15 +383,7 @@
             def _():
                 whiten_two(LEFT, 4 * c, 4 * c + 4)
 
-            def left_pair(n, carry):
-                own, t = n // 3, n % 3
-                y, code = partner(own, t, i)
-                real, imag = pair(w, LEFT + 2 * h + own, y, c * HR, HR)
-                sent_p[h, own, code, 0, c * HR:(c + 1) * HR, :] = real.astype(jnp.bfloat16)
-                sent_p[h, own, code, 1, c * HR:(c + 1) * HR, :] = imag.astype(jnp.bfloat16)
-                return carry
-
-            lax.fori_loop(0, 6, left_pair, 0)
+            left_products(LEFT + 2 * h, i, c * HR, HR, BW, sent_p.at[h])
             for n in range(2):
                 return_p(h, c, n).start()
 
@@ -351,7 +393,8 @@
         @pl.when(cut)
         def _():
             for n in range(2):
-                arrival(w.at[RIGHT + 2 + n, pl.ds(1, 2)], left_r.at[1, n]).wait_recv()
+                part = w.at[RIGHT + 2 + n, :, :, :, pl.ds(HB, HB)]
+                arrival(part, left_r.at[1, n]).wait_recv()
 
         @pl.when(jnp.logical_not(cut))
         def _():
@@ -416,18 +459,10 @@
     def half_products(c):
         i = CUT // 2
         for n in range(2):
-            part = w.at[HALF + n, pl.ds(0, 1), :, pl.ds(c * HR, HR)]
-            arrival(part, right_r.at[2, c, n]).wait_recv()
-
-        def half_pair(n, carry):
-            own, t = n // 3, n % 3
-            y, code = partner(own, t, i)
-            real, imag = pair(w, HALF + own, y, c * HR, HR, 1)
-            sent_m[own, code, 0, c * HR:(c + 1) * HR, :] = real.astype(jnp.bfloat16)
-            sent_m[own, code, 1, c * HR:(c + 1) * HR, :] = imag.astype(jnp.bfloat16)
-            return carry
-
-        lax.fori_loop(0, 6, half_pair, 0)
+            part = w.at[HALF + n, :, :, pl.ds(c * PR, PR), pl.ds(0, HB)]
+            arrival(part, half_r.at[c, n]).wait_recv()
+
+        left_products(HALF, i, c * PR, PR, HB, sent_m)
         for n in range(2):
             return_m(c, n).start()
 
@@ -466,7 +501,7 @@
 
     @pl.when(has_left & (k == 0))
     def _():
-        for c in range(2):
+        for c in range(PIECES):
             half_products(c)
 
     finish_q(0)
@@ -498,8 +533,8 @@
 
     @pl.when(has_right)
     def _():
-        for c in range(2):
-            arrival(got_m.at[:, :, pl.ds(c * HR, HR)], m_r.at[c]).wait_recv()
+        for c in range(PIECES):
+            arrival(got_m.at[:, :, pl.ds(c * PR, PR)], m_r.at[c]).wait_recv()
 
     pick[1] = cross[0, CUT, 0]
     pick[2] = cross[0, CUT, 1]
@@ -534,15 +569,17 @@
 
     @pl.when(has_left & (k == 0))
     def _():
-        for c in range(2):
+        for c in range(PIECES):
             for n in range(2):
                 return_m(c, n).wait_send()
 
     @pl.when(has_right)
     def _():
-        for b in range(CUT + 1):
+        for b in range(CUT):
             for c in range(2):
                 rightward(b, c).wait_send()
+        for c in range(PIECES):
+            half(c).wait_send()
         for h in range(2):
             hand_d(h, turn(h, k), o).wait_send()
 
@@ -585,11 +622,11 @@
             pltpu.VMEM((2, 3, 2, ST, ST), jnp.bfloat16),
             pltpu.VMEM((3, 2, ST, ST), jnp.bfloat16),
             dma((BANDS,)), dma((BANDS,)),
-            dma((4,)), dma((4,)), dma((2, 2)), dma((2, 2)), dma((5, 2)), dma((3, 2, 2)),
+            dma((4,)), dma((4,)), dma((2, 2)), dma((2, 2)), dma((4, 2)), dma((2, 2, 2)),
             dma((2, 4)), dma((8,)),
             dma((2, 2, 2)), dma((4, 2)), dma((2, 2)), dma((4,)),
             dma((4,)), dma((4,)), dma((2,)), dma((2,)),
-            dma((2, 2)), dma((2,)),
+            dma((PIECES,)), dma((PIECES, 2)), dma((PIECES, 2)), dma((PIECES,)),
             pltpu.SemaphoreType.REGULAR, pltpu.SemaphoreType.REGULAR,
         ],
         compiler_params=pltpu.CompilerParams(

time: 92.7 us -> 90.8 us (0.980)
  Pallas kernels: 88.7 us -> 87.1 us
    pallas_call x1, Pallas kernels: 88.7 us -> 87.1 us  [body(): pl.pallas_call(kernel, out_shape=pltpu.VMEM((SLOTS, BANDS, 2 * ST, ST), j...]
where the time goes in v8:
time: 90.8 us; the launch traced here: 89.4 us
  Pallas kernels  87.1 us (96%)
  local copies, waits for them, and re-layouts  2.36 us (3%)
    pallas_call x1, Pallas kernels, body(): pl.pallas_call(kernel, out_shape=pltpu.VMEM((SLOTS, BANDS, 2 * ST, ST), j...  87.1 us
    unnamed x1, local copies, waits for them, and re-layouts  2.36 us

profile of v8, /device:TPU:1, one launch (start us, length us, event | category | flops | bytes accessed | tf_op | source)
XLA Modules:
  0.0 89.4 jit_solution(11402250941027892211)
XLA Ops:
  0.0 87.1 %shard_map.46 = f32[5,8,256,128]{3,2,1,0:T(8,128)S(1)} custom-call(s32[5]{0:T(128)} %bitcast.11, s32[25,1,128]{2,1,0:T(1,128)} %bitcast.10, bf16[3,2,128,4096]{3,2,1,0:T(8,128)(2,1)} %bitcast.8, f32[5,8,256,128]{3,2,1,0:T(8,128)} %bitcast.9), custom_call_target="tpu_custom_call" | custom-call | tf_op jit(solution)/shard_map/pallas_call | solution.py:603
  87.1 2.4 %copy.6 = f32[1,1,5,8,2,128,128]{6,5,4,3,2,1,0:T(8,128)} copy(f32[1,1,5,8,2,128,128]{6,5,4,3,2,1,0:T(8,128)S(1)} %bitcast.7) | data formatting | bytes 10485760

commit v9 on v8

--- a/solution.py
+++ b/solution.py
@@ -29,19 +29,21 @@
 XLINE = 4
 
 
-def whiten(w, place, first=0, last=ST // 16):
+def whiten(w, place, first=0, last=ST // 16, source=None):
+    source = w.at[place] if source is None else source
+
     def rows_of(t, carry):
         rows = pl.ds(pl.multiple_of(t * 16, 16), 16)
         total = jnp.zeros((16, BW), jnp.float32)
         for s in range(SEG):
             for c in range(2):
-                x = w[place, s, c, rows, :].astype(jnp.float32)
+                x = source[s, c, rows, :].astype(jnp.float32)
                 total = total + x * x
         power = jnp.sum(total, axis=-1, keepdims=True) * (1.0 / (SEG * 2 * BW))
         gain = lax.rsqrt(power + EPSILON)
         for s in range(SEG):
             for c in range(2):
-                x = w[place, s, c, rows, :].astype(jnp.float32)
+                x = source[s, c, rows, :].astype(jnp.float32)
                 w[place, s, c, rows, :] = (x * gain).astype(jnp.bfloat16)
         return carry
 
@@ -84,12 +86,12 @@
 
 
 def kernel(
-    codes, bits, spectra, old, out,
-    w, cross, mask, pick, sent_p, got_p, sent_q, got_q, sent_m, got_m,
+    codes_in, bits_in, spectra, old, out,
+    w, raw, cross, mask, pick, sent_p, got_p, sent_q, got_q, sent_m, got_m,
     load_sem, old_sem,
     die_s, die_r, left_s, left_r, right_s, right_r, col_s, col_r,
     p_s, p_r, q_s, q_r, e_s, e_r, d_s, d_r,
-    half_s, half_r, m_s, m_r, ready_right, ready_below,
+    half_s, half_r, m_s, m_r, ready_right, ready_below, codes, bits, small_sem,
 ):
     gx = lax.axis_index("gx")
     gy = lax.axis_index("gy")
@@ -114,7 +116,8 @@
 
     def load(b):
         bins = pl.ds(b * BW, BW)
-        return pltpu.make_async_copy(spectra.at[:, :, :, bins], w.at[OWN + b], load_sem.at[b])
+        place = raw.at[RAW.index(b)] if b in RAW else w.at[OWN + b]
+        return pltpu.make_async_copy(spectra.at[:, :, :, bins], place, load_sem.at[b])
 
     def load_old(b):
         return pltpu.make_async_copy(old.at[:, b], out.at[:, b], old_sem.at[b])
@@ -131,7 +134,7 @@
             bins = pl.ds(HB, HB)
             src, dst = w.at[OWN + b, :, :, :, bins], w.at[at, :, :, :, bins]
         else:
-            src = spectra.at[:, :, :, pl.ds(b * BW, BW)] if b in RAW else w.at[OWN + b]
+            src = raw.at[RAW.index(b)] if b in RAW else w.at[OWN + b]
             dst = w.at[at]
         return remote(src, dst, left_s.at[h, j], left_r.at[h, k], base + j, left)
 
@@ -140,7 +143,7 @@
         h, j = b // 2, b % 2
         dst = w.at[LEFT + 2 * h + k, :, :, rows]
         if b in RAW:
-            src = spectra.at[:, :, rows, pl.ds(b * BW, BW)]
+            src = raw.at[RAW.index(b), :, :, rows]
         else:
             src = w.at[OWN + b, :, :, rows]
         return remote(src, dst, right_s.at[b, c], right_r.at[h, c, k], base + j, right)
@@ -196,6 +199,10 @@
     def arrival(dst, sem):
         return remote(dst, dst, load_sem.at[0], sem, base + o, gy)
 
+    small = (
+        pltpu.make_async_copy(codes_in, codes, small_sem.at[0]),
+        pltpu.make_async_copy(bits_in, bits, small_sem.at[1]),
+    )
     barrier = pltpu.get_barrier_semaphore()
 
     def greet(there, sem, row, col):
@@ -224,6 +231,9 @@
     greet(has_above, ready_below, above + 1, gy)
     greet(has_above & (k == 0), ready_below, above, gy)
 
+    for b in RAW:
+        load(b).wait()
+
     @pl.when(has_left)
     def _():
         leftward(5).start()
@@ -276,11 +286,16 @@
                     half(c).start()
 
     for n, b in enumerate(order):
-        load(b).wait()
-        whiten(w, OWN + b, 0, 4)
+        if b not in RAW:
+            load(b).wait()
+        source = raw.at[RAW.index(b)] if b in RAW else None
+        whiten(w, OWN + b, 0, 4, source)
         if n >= 1:
             send(order[n - 1])
-        whiten(w, OWN + b, 4, 8)
+        whiten(w, OWN + b, 4, 8, source)
+
+    for copy in small:
+        copy.start()
 
     def start_old(b, carry):
         load_old(b).start()
@@ -305,6 +320,8 @@
         def _():
             pass_on(a)
 
+    for copy in small:
+        copy.wait()
     column = lax.broadcasted_iota(jnp.int32, (ST, ST), 0)
     word = column // 30
     shift = column - word * 30
@@ -530,19 +547,27 @@
     lax.fori_loop(0, 4, finish_p, 0)
 
     await_q(2, CUT)
-
-    @pl.when(has_right)
-    def _():
-        for c in range(PIECES):
-            arrival(got_m.at[:, :, pl.ds(c * PR, PR)], m_r.at[c]).wait_recv()
-
+    load_old(CUT).wait()
     pick[1] = cross[0, CUT, 0]
     pick[2] = cross[0, CUT, 1]
+    near = got_q[2].astype(jnp.float32)
     for n in range(3):
-        partial = got_m[n].reshape(2 * ST, ST).astype(jnp.float32)
-        near = got_q[2].astype(jnp.float32)
-        pick[3 + n] = partial + jnp.where(k * 2 == n, near, cross[0, CUT, 2 + n])
-    combine(CUT)
+        pick[3 + n] = jnp.where(k * 2 == n, near, cross[0, CUT, 2 + n])
+
+    for c in range(PIECES):
+
+        @pl.when(has_right)
+        def _():
+            arrival(got_m.at[:, :, pl.ds(c * PR, PR)], m_r.at[c]).wait_recv()
+
+        for part in range(2):
+            rows = slice(c * PR, (c + 1) * PR)
+            both = slice(part * ST + c * PR, part * ST + (c + 1) * PR)
+            for n in range(3):
+                pick[3 + n, both] = pick[3 + n, both] + got_m[n, part, rows].astype(jnp.float32)
+            for s in range(SLOTS):
+                which = codes[s] + 1
+                out[s, CUT, both] = out[s, CUT, both] + mask[s, rows] * pick[which, both]
 
     for i in range(4):
         die(i).wait_send()
@@ -604,14 +629,15 @@
         kernel,
         out_shape=pltpu.VMEM((SLOTS, BANDS, 2 * ST, ST), jnp.float32),
         in_specs=[
-            pl.BlockSpec(memory_space=pltpu.SMEM),
-            pl.BlockSpec(memory_space=pltpu.VMEM),
+            pl.BlockSpec(memory_space=pl.ANY),
+            pl.BlockSpec(memory_space=pl.ANY),
             pl.BlockSpec(memory_space=pl.ANY),
             pl.BlockSpec(memory_space=pl.ANY),
         ],
         out_specs=pl.BlockSpec(memory_space=pltpu.VMEM),
         scratch_shapes=[
             pltpu.VMEM((PLACES, SEG, 2, ST, BW), jnp.bfloat16),
+            pltpu.VMEM((len(RAW), SEG, 2, ST, BW), jnp.bfloat16),
             pltpu.VMEM((2, BANDS, SLOTS, 2 * ST, ST), jnp.float32),
             pltpu.VMEM((SLOTS, ST, ST), jnp.float32),
             pltpu.VMEM((SLOTS + 1, 2 * ST, ST), jnp.float32),
@@ -628,6 +654,9 @@
             dma((4,)), dma((4,)), dma((2,)), dma((2,)),
             dma((PIECES,)), dma((PIECES, 2)), dma((PIECES, 2)), dma((PIECES,)),
             pltpu.SemaphoreType.REGULAR, pltpu.SemaphoreType.REGULAR,
+            pltpu.SMEM((SLOTS,), jnp.int32),
+            pltpu.VMEM((SLOTS * WORDS, 1, ST), jnp.int32),
+            dma((2,)),
         ],
         compiler_params=pltpu.CompilerParams(
             collective_id=0, has_side_effects=True, vmem_limit_bytes=52 * 1024 * 1024

time: 90.8 us -> 89.7 us (0.988)
  Pallas kernels: 87.1 us -> 86 us
    pallas_call x1, Pallas kernels: 87.1 us -> 86 us  [body(): pl.pallas_call(kernel, out_shape=pltpu.VMEM((SLOTS, BANDS, 2 * ST, ST), j...]
where the time goes in v9:
time: 89.7 us; the launch traced here: 88.4 us
  Pallas kernels  86 us (96%)
  local copies, waits for them, and re-layouts  2.36 us (3%)
    pallas_call x1, Pallas kernels, body(): pl.pallas_call(kernel, out_shape=pltpu.VMEM((SLOTS, BANDS, 2 * ST, ST), j...  86 us
    unnamed x1, local copies, waits for them, and re-layouts  2.36 us

profile of v9, /device:TPU:1, one launch (start us, length us, event | category | flops | bytes accessed | tf_op | source)
XLA Modules:
  0.0 88.4 jit_solution(1179254462527267530)
XLA Ops:
  0.0 86.0 %shard_map.46 = f32[5,8,256,128]{3,2,1,0:T(8,128)S(1)} custom-call(s32[5]{0:T(128)} %bitcast.11, s32[25,1,128]{2,1,0:T(1,128)} %bitcast.10, bf16[3,2,128,4096]{3,2,1,0:T(8,128)(2,1)} %bitcast.8, f32[5,8,256,128]{3,2,1,0:T(8,128)} %bitcast.9), custom_call_target="tpu_custom_call" | custom-call | tf_op jit(solution)/shard_map/pallas_call | solution.py:628
  86.0 2.4 %copy.6 = f32[1,1,5,8,2,128,128]{6,5,4,3,2,1,0:T(8,128)} copy(f32[1,1,5,8,2,128,128]{6,5,4,3,2,1,0:T(8,128)S(1)} %bitcast.7) | data formatting | bytes 10485760

commit v10 on v9

--- a/solution.py
+++ b/solution.py
@@ -103,8 +103,8 @@
     above = lax.rem(base + ROWS - 2, ROWS)
     below = lax.rem(base + 2, ROWS)
     has_left, has_right = gy > 0, gy < COLS - 1
-    wrap_left = has_left & (lax.rem(gy, XLINE) == 0)
-    wrap_right = has_right & (lax.rem(gy, XLINE) == XLINE - 1)
+    wrap_left = has_left
+    wrap_right = has_right
     has_above, has_below = base > 0, base < ROWS - 2
     swaps = jnp.where(k == 0, base > 0, base < ROWS - 2)
 

time: 89.7 us -> 89.7 us (level)
  no operation moved by 1% of the time
where the time goes in v10:
time: 89.7 us; the launch traced here: 88.4 us
  Pallas kernels  86.1 us (96%)
  local copies, waits for them, and re-layouts  2.36 us (3%)
    pallas_call x1, Pallas kernels, body(): pl.pallas_call(kernel, out_shape=pltpu.VMEM((SLOTS, BANDS, 2 * ST, ST), j...  86.1 us
    unnamed x1, local copies, waits for them, and re-layouts  2.36 us

profile of v10, /device:TPU:1, one launch (start us, length us, event | category | flops | bytes accessed | tf_op | source)
XLA Modules:
  0.0 88.4 jit_solution(1923957385406038600)
XLA Ops:
  0.0 86.1 %shard_map.46 = f32[5,8,256,128]{3,2,1,0:T(8,128)S(1)} custom-call(s32[5]{0:T(128)} %bitcast.11, s32[25,1,128]{2,1,0:T(1,128)} %bitcast.10, bf16[3,2,128,4096]{3,2,1,0:T(8,128)(2,1)} %bitcast.8, f32[5,8,256,128]{3,2,1,0:T(8,128)} %bitcast.9), custom_call_target="tpu_custom_call" | custom-call | tf_op jit(solution)/shard_map/pallas_call | solution.py:628
  86.1 2.4 %copy.6 = f32[1,1,5,8,2,128,128]{6,5,4,3,2,1,0:T(8,128)} copy(f32[1,1,5,8,2,128,128]{6,5,4,3,2,1,0:T(8,128)S(1)} %bitcast.7) | data formatting | bytes 10485760
